TPU v7x, 128 devices: a whole 4x4x4 slice. The times are simulated.
128 devices in a mesh: branch: 16 (over z, x), group: 8 (over y, core).
Axes of the slice: x: 4, y: 4, z: 4, core: 2. Of those that a mesh axis runs over, the one named last changes fastest.
Arguments:
- basis: float32 [2, 131072, 256], P(None, ('branch', 'group')), may hold values from -8 to 8
- spread_owner: int32 [131072, 2], P(('branch', 'group')), may hold values from 0 to 127, all different within a row; in each aligned block of 1024 rows (0 to 1023, 1024 to 2047, ...) at most 32 rows name the same one
- spread_row: int32 [131072, 2], P(('branch', 'group')), may hold values from 0 to 1023
- spread_weight: float32 [131072, 2], P(('branch', 'group')), may hold values from 0.2 to 1
- gram_term: bfloat16 [256, 512, 512], P(('branch', 'group')), may hold values from -0.25 to 0.25
- near_block: bfloat16 [256, 8, 512, 512], P(('branch', 'group')), may hold values from -0.09375 to 0.09375
- near_list: int32 [256, 8], P(('branch', 'group')), may hold values from 0 to 1
- leaf_basis: bfloat16 [256, 64, 512], P(('branch', 'group')), may hold values from -0.25 to 0.25
- far_block: bfloat16 [256, 16, 64, 64], P(('branch', 'group')), may hold values from -0.1875 to 0.1875
- far_list: int32 [256, 16], P(('branch', 'group')), may hold values from 0 to 31
- ascend: bfloat16 [256, 64, 64], P(('branch', 'group')), may hold values from -0.125 to 0.125
- descend: bfloat16 [256, 64, 64], P(('branch', 'group')), may hold values from -0.75 to 0.75
- top_block: bfloat16 [512, 512], P('group'), may hold values from -0.25 to 0.25
Outputs:
- next_vector: float32 [131072, 256], P(('branch', 'group'))
- hessenberg: float32 [3, 256], replicated
Inputs may be any that keep to these rules, and one draw needn't show every extreme that they name: `spread_owner`: within the rows of one device no owner is named by more than 32 entries, and one row never names an owner twice.
All inputs are finite; a program needn't handle non-finite values.
Results may differ from a plain program's by a relative error of at most 0.0035.
Values may be sent and summed in bfloat16 or wider, within the bound.
A program may use at most 64 MiB of HBM per device.

v0:
```python
import functools

import jax
import jax.numpy as jnp
from jax import lax
from jax.sharding import Mesh
from jax.sharding import PartitionSpec as P

BRANCH = ("branch_0", "branch_1")
GROUP = ("group_0", "group_1")
BRANCH_GROUP = ("branch_0", "branch_1", "group_0", "group_1")


def laid_out(pieces, dim):
    shape = list(pieces.shape[1:])
    shape[dim] *= pieces.shape[0]
    return jnp.moveaxis(pieces, 0, dim).reshape(shape)


def copy_for_each(shard, axis):
    copies = jnp.broadcast_to(shard, (lax.axis_size(axis), *shard.shape))
    return lax.all_to_all(copies, axis, split_axis=0, concat_axis=0, tiled=True)


def collect(shard, axis, dim):
    return laid_out(copy_for_each(shard, axis), dim)


def over_copies(shard, axis):
    everything = copy_for_each(shard, axis)
    return jnp.sum(everything, axis=0)


def by_axis(shard, axes):
    return functools.reduce(lax.psum, axes, shard)


def rounded(values):
    return values.astype(jnp.bfloat16)


def contract(pattern, first_op, second_op):
    return jnp.einsum(pattern, first_op, second_op, preferred_element_type=jnp.float32)


def body(
    basis,
    spread_owner,
    spread_row,
    spread_weight,
    gram_term,
    near_block,
    near_list,
    leaf_basis,
    far_block,
    far_list,
    ascend,
    descend,
    top_block,
):
    branches = lax.axis_size(BRANCH)
    groups = lax.axis_size(GROUP)
    devices = branches * groups
    leaves = gram_term.shape[0]
    leaf_size = gram_term.shape[1]
    rows_dev = basis.shape[1]
    columns = basis.shape[2]
    spread = spread_owner.shape[1]
    slot_count = 2 * spread * rows_dev // devices
    vector = basis[basis.shape[0] - 1]
    owners = spread_owner.reshape(-1)
    weights = spread_weight.reshape(-1)
    onehot = (owners[:, None] == jnp.arange(devices, dtype=jnp.int32)[None, :]).astype(jnp.int32)
    slot_index = jnp.sum(jnp.cumsum(onehot, axis=0) * onehot, axis=1) - 1
    position = owners * slot_count + slot_index
    entries = jnp.repeat(vector, spread, axis=0) * weights[:, None]
    send_values = jnp.zeros((devices * slot_count, columns), jnp.float32).at[position].set(entries)
    send_rows = (
        jnp.zeros((devices * slot_count,), jnp.float32)
        .at[position]
        .set(spread_row.reshape(-1).astype(jnp.float32))
    )
    got_values, got_rows = (
        lax.all_to_all(
            send_values.reshape(devices, slot_count, columns),
            BRANCH_GROUP,
            split_axis=0,
            concat_axis=0,
            tiled=True,
        ),
        lax.all_to_all(
            send_rows.reshape(devices, slot_count),
            BRANCH_GROUP,
            split_axis=0,
            concat_axis=0,
            tiled=True,
        ),
    )
    got_rows = got_rows.reshape(-1).astype(jnp.int32)
    dual_in = (
        jnp.zeros((rows_dev, columns), jnp.float32)
        .at[got_rows]
        .add(got_values.reshape(-1, columns))
    )
    dual_split = dual_in.reshape(leaves, leaf_size, columns)
    first_pass = dual_split + contract("lji,ljc->lic", gram_term, rounded(dual_split))
    first_low = rounded(first_pass)
    near_sum = contract("lkij,lkjc->lic", near_block, first_low[near_list])
    leaf_coeff = contract("lri,lic->lrc", leaf_basis, first_low)
    coeff_low = rounded(leaf_coeff)
    partial_value = contract("lrs,lsc->rc", ascend, coeff_low)
    gathered_low = collect(coeff_low, BRANCH, 0)
    parent = over_copies(partial_value, BRANCH)
    parent_low = rounded(parent)
    top_field = jnp.dot(
        top_block, collect(parent_low, GROUP, 0), preferred_element_type=jnp.float32
    )
    far_sum = contract("lkrs,lksc->lrc", far_block, gathered_low[far_list])
    descent = far_sum + contract("lrs,sc->lrc", descend, rounded(top_field))
    dual_image = first_pass + near_sum + contract("lri,lrc->lic", leaf_basis, rounded(descent))
    dual_out = (dual_image + contract("lij,ljc->lic", gram_term, rounded(dual_image))).reshape(
        rows_dev, columns
    )
    replies = dual_out[got_rows]
    returned = lax.all_to_all(
        replies.reshape(devices, slot_count, columns),
        BRANCH_GROUP,
        split_axis=0,
        concat_axis=0,
        tiled=True,
    )
    returned = returned.reshape(devices * slot_count, columns)
    image_primal = jnp.sum(
        (returned[position] * weights[:, None]).reshape(rows_dev, spread, columns), axis=1
    )
    total_rows = rows_dev * devices
    cross_sum, self_sum, mutual = (
        by_axis(jnp.sum(basis * image_primal[None], axis=1), BRANCH_GROUP),
        by_axis(jnp.sum(image_primal * image_primal, axis=0), BRANCH_GROUP),
        by_axis(jnp.sum(basis[:, None] * basis[None], axis=2), BRANCH_GROUP),
    )
    projection = cross_sum / total_rows
    remainder = image_primal - jnp.sum(projection[:, None, :] * basis, axis=0)
    square = (
        self_sum / total_rows
        - 2.0 * jnp.sum(projection * projection, axis=0)
        + jnp.sum(projection[:, None] * projection[None] * mutual, axis=(0, 1)) / total_rows
    )
    norm_scale = jnp.sqrt(square + 1e-06)
    return (remainder / norm_scale, jnp.concatenate([projection, norm_scale[None]], axis=0))


def solution(mesh):
    finer = Mesh(mesh.devices.reshape(4, 4, 4, 2), ("branch_0", "branch_1", "group_0", "group_1"))
    return jax.shard_map(
        body,
        mesh=finer,
        in_specs=(
            P(None, BRANCH_GROUP, None),
            P(BRANCH_GROUP, None),
            P(BRANCH_GROUP, None),
            P(BRANCH_GROUP, None),
            P(BRANCH_GROUP, None, None),
            P(BRANCH_GROUP, None, None, None),
            P(BRANCH_GROUP, None),
            P(BRANCH_GROUP, None, None),
            P(BRANCH_GROUP, None, None, None),
            P(BRANCH_GROUP, None),
            P(BRANCH_GROUP, None, None),
            P(BRANCH_GROUP, None, None),
            P(GROUP, None),
        ),
        out_specs=(P(BRANCH_GROUP, None), P()),
        check_vma=False,
    )
```

profile of v0, /device:TPU:1, one launch (start us, length us, event | category | flops | bytes accessed | tf_op | source)
XLA Modules:
  0.0 334.2 jit_solution(11335173466064759379)
XLA Ops:
  7.7 1.4 mul.97
  10.1 1.3 reshape.170
  11.4 8.1 %scatter_custom_fusion = f32[4096]{0:T(1024)S(1)} fusion(s32[2048]{0:T(1024)S(1)} %bitcast.90, f32[2048]{0:T(1024)S(1)} %reshape.170, f32[]{:T(128)} %constant.10.clone.1), kind=kCustom, calls=%fused_computation.52 | custom fusion | bytes 16388 | tf_op jit(solution)/shard_map/scatter | solution.py:81
  20.2 11.5 %all-to-all-start = ((f32[128,1,32]{2,1,0:T(1,128)}), f32[128,1,32]{2,1,0:T(1,128)S(1)}, u32[]{:S(2)}, u32[]{:S(2)}) async-start(f32[128,1,32]{2,1,0:T(1,128)} %bitcast.5), calls=%async_computation | async-start | bytes 131072 | tf_op jit(solution)/shard_map/all_to_all | solution.py:91
  33.8 3.3 broadcast_in_dim.46
  37.1 2.7 reshape.125
  39.8 12.2 %scatter_custom_fusion.1 = f32[4096,256]{1,0:T(8,128)} fusion(s32[2048]{0:T(1024)S(1)} %bitcast.91, f32[2048,256]{1,0:T(8,128)S(1)} %reshape.125, f32[]{:T(128)} %constant.10.clone.1, f32[2048]{0:T(1024)S(1)} %mul.99), kind=kCustom, calls=%fused_computation.11 | custom fusion | flops 524288 | bytes 6299652 | tf_op jit(solution)/shard_map/scatter | solution.py:77
  52.0 10.2 %all-to-all-start.1 = ((f32[128,32,256]{2,1,0:T(8,128)}), f32[128,32,256]{2,1,0:T(8,128)}, u32[]{:S(2)}, u32[]{:S(2)}) async-start(f32[128,32,256]{2,1,0:T(8,128)} %bitcast.82), calls=%async_computation.1 | async-start | bytes 8388608 | tf_op jit(solution)/shard_map/all_to_all | solution.py:84
  62.6 52.4 %all-to-all-done.1 = f32[128,32,256]{2,1,0:T(8,128)} async-done(((f32[128,32,256]{2,1,0:T(8,128)}), f32[128,32,256]{2,1,0:T(8,128)}, u32[]{:S(2)}, u32[]{:S(2)}) %all-to-all-start.1) | async-done | bytes 4194336 | tf_op jit(solution)/shard_map/all_to_all | solution.py:84
  115.0 24.0 %scatter_custom_fusion.2 = f32[1024,256]{1,0:T(8,128)S(1)} fusion(s32[4096]{0:T(1024)S(1)} %bitcast.88, f32[4096,256]{1,0:T(8,128)} %bitcast.9, f32[]{:T(128)} %constant.10.clone.1), kind=kCustom, calls=%fused_computation.45 | custom fusion | flops 1048576 | bytes 1049088 | tf_op jit(solution)/shard_map/scatter-add | solution.py:103
  140.3 2.7 fusion.22
  143.6 18.4 %all_to_all.34 = f32[16,64,256]{2,1,0:T(8,128)S(1)} all-to-all(f32[16,64,256]{2,1,0:T(8,128)S(1)} %broadcast_in_dim.50), channel_id=1, replica_groups=mesh['branch_0'=4,'branch_1'=4,'group_0'=4,'group_1'=2] {'branch_0','bra..., dimensions={0} | all-to-all | bytes 2097152 | tf_op jit(solution)/shard_map/all_to_all | solution.py:22
  163.1 4.4 %all-to-all-start.2 = ((bf16[16,2,64,256]{3,2,1,0:T(8,128)(2,1)}), bf16[16,2,64,256]{3,2,1,0:T(8,128)(2,1)}, u32[]{:S(2)}, u32[]{:S(2)}) async-start(bf16[16,2,64,256]{3,2,1,0:T(8,128)(2,1)} %broadcast_in_dim.48), calls=%async_computation.2 | async-start | bytes 2097152 | tf_op jit(solution)/shard_map/all_to_all | solution.py:22
  168.3 2.7 gather_fusion
  171.1 11.4 %all-to-all-done.2 = bf16[16,2,64,256]{3,2,1,0:T(8,128)(2,1)} async-done(((bf16[16,2,64,256]{3,2,1,0:T(8,128)(2,1)}), bf16[16,2,64,256]{3,2,1,0:T(8,128)(2,1)}, u32[]{:S(2)}, u32[]{:S(2)}) %all-to-all-start.2) | async-done | bytes 1048608 | tf_op jit(solution)/shard_map/all_to_all | solution.py:22
  183.2 6.8 %all-to-all-start.4 = ((bf16[8,64,256]{2,1,0:T(8,128)(2,1)}), bf16[8,64,256]{2,1,0:T(8,128)(2,1)S(1)}, u32[]{:S(2)}, u32[]{:S(2)}) async-start(bf16[8,64,256]{2,1,0:T(8,128)(2,1)} %broadcast_in_dim.51), calls=%async_computation.4 | async-start | bytes 524288 | tf_op jit(solution)/shard_map/all_to_all | solution.py:22
  190.0 7.2 %fusion.6 = f32[2,512,256]{1,2,0:T(8,128)S(1)} fusion(f32[2,512,256]{1,2,0:T(8,128)} %get-tuple-element.17, bf16[2,8,512,256]{2,3,1,0:T(8,128)(2,1)} %bitcast.85, bf16[2,8,512,512]{3,2,1,0:T(8,128)(2,1)} %param.18), kind=kOutput, calls=%fused_computation.21 | convolution fusion | flops 2147745792 | bytes 14680064 | tf_op jit(solution)/shard_map/lkij,lkjc->lic/dot_general | solution.py:43
  197.2 2.0 gather_fusion.1
  199.2 2.0 convolution_bitcast_fusion.4
  201.2 1.6 fusion.10
  202.8 1.4 fusion.3
  205.0 16.1 %gather_fusion.2 = f32[4096,256]{1,0:T(8,128)} fusion(f32[1024,256]{1,0:T(8,128)S(1)} %bitcast.80, s32[4096]{0:T(1024)S(1)} %broadcast_clamp_fusion), kind=kCustom, calls=%fused_computation.2 | custom fusion | bytes 8404992 | tf_op jit(solution)/shard_map/gather | solution.py:124
  221.1 6.0 %all-to-all-start.5 = ((f32[128,32,256]{2,1,0:T(8,128)}), f32[128,32,256]{2,1,0:T(8,128)}, u32[]{:S(2)}, u32[]{:S(2)}) async-start(f32[128,32,256]{2,1,0:T(8,128)} %bitcast.81), calls=%async_computation.5 | async-start | bytes 8388608 | tf_op jit(solution)/shard_map/all_to_all | solution.py:125
  227.5 52.4 %all-to-all-done.5 = f32[128,32,256]{2,1,0:T(8,128)} async-done(((f32[128,32,256]{2,1,0:T(8,128)}), f32[128,32,256]{2,1,0:T(8,128)}, u32[]{:S(2)}, u32[]{:S(2)}) %all-to-all-start.5) | async-done | bytes 4194336 | tf_op jit(solution)/shard_map/all_to_all | solution.py:125
  279.9 10.8 %gather_fusion.3 = f32[2048,256]{1,0:T(8,128)} fusion(f32[4096,256]{1,0:T(8,128)} %bitcast.31, s32[2048]{0:T(1024)S(1)} %broadcast_clamp_fusion.1), kind=kCustom, calls=%fused_computation.3 | custom fusion | bytes 4202496 | tf_op jit(solution)/shard_map/gather | solution.py:134
  290.6 3.5 %gather.18 = f32[1024,2,256]{2,1,0:T(2,128)} reshape(f32[2048,256]{1,0:T(8,128)} %gather_fusion.3) | data formatting | bytes 4194304 | tf_op jit(solution)/shard_map/gather | solution.py:134
  294.2 6.9 %multiply_reduce_fusion.3 = f32[1024,256]{1,0:T(8,128)S(1)} fusion(f32[1024,2,256]{2,1,0:T(2,128)} %gather.18, f32[1024,2]{1,0:T(8,128)} %copy-done.4), kind=kLoop, calls=%fused_computation.10 | loop fusion | flops 786432 | bytes 3153920 | tf_op jit(solution)/shard_map/reduce_sum | solution.py:133
  302.1 6.7 %all-reduce.2 = (f32[2,256]{1,0:T(2,128)S(1)}, f32[2,2,256]{2,1,0:T(2,128)S(1)}, f32[256]{0:T(256)S(1)}) all-reduce(f32[2,256]{1,0:T(2,128)S(1)} %multiply_reduce_fusion.2, f32[2,2,256]{2,1,0:T(2,128)S(1)} %multiply_reduce_fusion, ...), channel_id=1, replica_groups=mesh['branch_0'=4,'branch_1'=4,'group_0'=4,'group_1'=2] {'branch_0'}, use_global_device_ids=true, to_apply=%region_9.10 | all-reduce | flops 1792 | bytes 14336 | tf_op jit(solution)/shard_map/psum | solution.py:35
  308.9 7.0 %all-reduce.1 = (f32[2,256]{1,0:T(2,128)S(1)}, f32[2,2,256]{2,1,0:T(2,128)S(1)}, f32[256]{0:T(256)S(1)}) all-reduce(f32[2,256]{1,0:T(2,128)S(1)} %get-tuple-element.8, f32[2,2,256]{2,1,0:T(2,128)S(1)} %get-tuple-element.9, f32[256]{0:T(256)S(1)} %get-tuple-element.10), channel_id=1, replica_groups=mesh['branch_0'=4,'branch_1'=4,'group_0'=4,'group_1'=2] {'branch_1'}, use_global_device_ids=true, to_apply=%region_10.11 | all-reduce | flops 1792 | bytes 14336 | tf_op jit(solution)/shard_map/psum | solution.py:35
  315.9 6.2 %all-reduce = (f32[2,256]{1,0:T(2,128)S(1)}, f32[2,2,256]{2,1,0:T(2,128)S(1)}, f32[256]{0:T(256)S(1)}) all-reduce(f32[2,256]{1,0:T(2,128)S(1)} %get-tuple-element.5, f32[2,2,256]{2,1,0:T(2,128)S(1)} %get-tuple-element.6, f32[256]{0:T(256)S(1)} %get-tuple-element.7), channel_id=1, replica_groups=mesh['branch_0'=4,'branch_1'=4,'group_0'=4,'group_1'=2] {'group_0'}, use_global_device_ids=true, to_apply=%region_11.12 | all-reduce | flops 1792 | bytes 14336 | tf_op jit(solution)/shard_map/psum | solution.py:35
  322.1 8.9 %all-reduce.3 = (f32[2,256]{1,0:T(2,128)S(1)}, f32[2,2,256]{2,1,0:T(2,128)S(1)}, f32[256]{0:T(256)S(1)}) all-reduce(f32[2,256]{1,0:T(2,128)S(1)} %get-tuple-element.2, f32[2,2,256]{2,1,0:T(2,128)S(1)} %get-tuple-element.3, f32[256]{0:T(256)S(1)} %get-tuple-element.4), channel_id=1, replica_groups=mesh['branch_0'=4,'branch_1'=4,'group_0'=4,'group_1'=2] {'group_1'}, use_global_device_ids=true, to_apply=%region_12.13 | all-reduce | flops 1792 | bytes 14336 | tf_op jit(solution)/shard_map/psum | solution.py:35
  331.9 2.3 subtract_divide_fusion
  (79 shorter events, 18.8 us)
Async XLA Ops:
  0.6 139.7 %copy-start = (bf16[2,512,512]{2,1,0:T(8,128)(2,1)S(1)}, bf16[2,512,512]{2,1,0:T(8,128)(2,1)}, u32[]{:S(2)}) copy-start(bf16[2,512,512]{2,1,0:T(8,128)(2,1)} %param.17) | copy-start | bytes 3145732
  1.9 7.1 %copy-start.11 = (s32[1024,2]{0,1:T(2,128)S(1)}, s32[1024,2]{0,1:T(2,128)}, u32[]{:S(2)}) copy-start(s32[1024,2]{0,1:T(2,128)} %param.15) | copy-start | bytes 24580
  3.0 28.7 %copy-start.1 = (f32[2,1024,256]{2,1,0:T(8,128)S(1)}, f32[2,1024,256]{2,1,0:T(8,128)}, u32[]{:S(2)}) copy-start(f32[2,1024,256]{2,1,0:T(8,128)} %param.13) | copy-start | bytes 6291460
  3.4 1.0 copy-start.5
  5.7 27.1 %copy-start.10 = (f32[1024,2]{0,1:T(2,128)S(1)}, f32[1024,2]{0,1:T(2,128)}, u32[]{:S(2)}) copy-start(f32[1024,2]{0,1:T(2,128)} %param.16) | copy-start | bytes 24580
  11.4 28.4 %copy-start.8 = (s32[2048,1]{0,1:T(1,128)}, s32[2048,1]{0,1:T(1,128)S(1)}, u32[]{:S(2)}) copy-start(s32[2048,1]{0,1:T(1,128)S(1)} %compare_select_fusion.1) | copy-start | bytes 24580
  20.2 31.8 %all-to-all-start = ((f32[128,1,32]{2,1,0:T(1,128)}), f32[128,1,32]{2,1,0:T(1,128)S(1)}, u32[]{:S(2)}, u32[]{:S(2)}) async-start(f32[128,1,32]{2,1,0:T(1,128)} %bitcast.5), calls=%async_computation | async-start | bytes 131072 | tf_op jit(solution)/shard_map/all_to_all | solution.py:91
  33.0 0.9 copy-start.4
  52.0 62.9 %all-to-all-start.1 = ((f32[128,32,256]{2,1,0:T(8,128)}), f32[128,32,256]{2,1,0:T(8,128)}, u32[]{:S(2)}, u32[]{:S(2)}) async-start(f32[128,32,256]{2,1,0:T(8,128)} %bitcast.82), calls=%async_computation.1 | async-start | bytes 8388608 | tf_op jit(solution)/shard_map/all_to_all | solution.py:84
  62.3 80.8 %copy-start.6 = (bf16[2,64,512]{2,1,0:T(8,128)(2,1)S(1)}, bf16[2,64,512]{2,1,0:T(8,128)(2,1)}, u32[]{:S(2)}) copy-start(bf16[2,64,512]{2,1,0:T(8,128)(2,1)} %param.20) | copy-start | bytes 393220
  115.0 28.3 %copy-start.7 = (bf16[2,64,64]{2,1,0:T(8,128)(2,1)S(1)}, bf16[2,64,64]{2,1,0:T(8,128)(2,1)}, u32[]{:S(2)}) copy-start(bf16[2,64,64]{2,1,0:T(8,128)(2,1)} %param.23) | copy-start | bytes 49156
  143.0 24.5 %copy-start.12 = (s32[2,8]{1,0:T(2,128)S(1)}, s32[2,8]{1,0:T(2,128)}, u32[]{:S(2)}) copy-start(s32[2,8]{1,0:T(2,128)} %param.19) | copy-start | bytes 196
  143.0 24.6 %copy-start.13 = (s32[2,16]{1,0:T(2,128)S(1)}, s32[2,16]{1,0:T(2,128)}, u32[]{:S(2)}) copy-start(s32[2,16]{1,0:T(2,128)} %param.22) | copy-start | bytes 388
  163.1 19.3 %all-to-all-start.2 = ((bf16[16,2,64,256]{3,2,1,0:T(8,128)(2,1)}), bf16[16,2,64,256]{3,2,1,0:T(8,128)(2,1)}, u32[]{:S(2)}, u32[]{:S(2)}) async-start(bf16[16,2,64,256]{3,2,1,0:T(8,128)(2,1)} %broadcast_in_dim.48), calls=%async_computation.2 | async-start | bytes 2097152 | tf_op jit(solution)/shard_map/all_to_all | solution.py:22
  183.2 18.0 %all-to-all-start.4 = ((bf16[8,64,256]{2,1,0:T(8,128)(2,1)}), bf16[8,64,256]{2,1,0:T(8,128)(2,1)S(1)}, u32[]{:S(2)}, u32[]{:S(2)}) async-start(bf16[8,64,256]{2,1,0:T(8,128)(2,1)} %broadcast_in_dim.51), calls=%async_computation.4 | async-start | bytes 524288 | tf_op jit(solution)/shard_map/all_to_all | solution.py:22
  221.1 6.1 %copy-start.9 = (s32[2048,1]{0,1:T(1,128)S(1)}, s32[2048,1]{0,1:T(1,128)}, u32[]{:S(2)}) copy-start(s32[2048,1]{0,1:T(1,128)} %copy-done.8) | copy-start | bytes 24580
  221.1 6.1 %copy-start.2 = (f32[2,1024,256]{2,1,0:T(8,128)S(1)}, f32[2,1024,256]{2,1,0:T(8,128)}, u32[]{:S(2)}) copy-start(f32[2,1024,256]{2,1,0:T(8,128)} %param.13) | copy-start | bytes 6291460
  221.1 58.8 %all-to-all-start.5 = ((f32[128,32,256]{2,1,0:T(8,128)}), f32[128,32,256]{2,1,0:T(8,128)}, u32[]{:S(2)}, u32[]{:S(2)}) async-start(f32[128,32,256]{2,1,0:T(8,128)} %bitcast.81), calls=%async_computation.5 | async-start | bytes 8388608 | tf_op jit(solution)/shard_map/all_to_all | solution.py:125
  301.0 1.0 copy-start.3
where the time goes:
time: 336 us; the launch traced here: 334 us
  waiting for transfers between devices  116 us (35%)
  local copies, waits for them, and re-layouts  64.1 us (19%)
  other arithmetic  50.9 us (15%)
  blocking collectives  47.2 us (14%)
  starting transfers between devices  38.9 us (12%)
  matrix products  15.8 us (5%)
    all_to_all x1, waiting for transfers between devices, body(): lax.all_to_all(replies.reshape(devices, slot_count, columns), BRANCH_GROU...  52.4 us
    all_to_all x1, waiting for transfers between devices, body(): lax.all_to_all(send_values.reshape(devices, slot_count, columns), BRANCH_...  52.4 us
    psum x4, blocking collectives, by_axis(): return functools.reduce(lax.psum, axes, shard)  28.9 us
    scatter-add x1, other arithmetic, body(): dual_in = jnp.zeros((rows_dev, columns), jnp.float32).at[got_rows].add(go...  24 us
    all_to_all x1, blocking collectives, copy_for_each(): return lax.all_to_all(copies, axis, split_axis=0, concat_axis=0, tiled=True)  18.4 us
    gather x1, local copies, waits for them, and re-layouts, body(): replies = dual_out[got_rows]  16.1 us
    gather x2, local copies, waits for them, and re-layouts, body(): returned[position] * weights[:, None]  14.3 us
    dot_general x7, matrix products, contract(): jnp.einsum(pattern, first_op, second_op, preferred_element_type=jnp.float32)  14.2 us
  transfers between devices with their start and end apart: 5, of which 3 were waited for; matrix products, arithmetic and copies ran while one was open for 10% of the time, Pallas kernels for 0%

commit v1 on v0

v1 whole, which is shorter than its diff:
```python
import jax
import jax.numpy as jnp
from jax import lax
from jax.experimental import pallas as pl
from jax.experimental.pallas import tpu as pltpu
from jax.sharding import Mesh
from jax.sharding import PartitionSpec as P

AXES = ("branch_0", "branch_1", "group_0", "group_1")
BRANCH_GROUP = AXES
GROUP = AXES[2:]
MESH = pl.DeviceIdType.MESH
F32 = jnp.float32
BF16 = jnp.bfloat16
DEV = 128
SLOTS = 32
ROWS = 1024
LEAF = 512
RANK = 64
COLS = 256
TOTAL = DEV * ROWS
SELF = 2


def dot(a, b):
    return jnp.dot(a, b, preferred_element_type=F32)


def dot_t(a, b):
    return lax.dot_general(a, b, (((0,), (0,)), ((), ())), preferred_element_type=F32)


def kernel(
    owner_ref, row_ref, weight_ref, near_list, far_list, top_ref,
    basis_hbm, gram_hbm, near_hbm, base_hbm, far_hbm, asc_hbm, desc_hbm,
    out_ref, hess_ref,
    basis, gram, near, base, far, asc, desc,
    rank_of, weight_hi, weight_lo, row_of,
    pick_hi, pick_lo, place,
    vec_hi, vec_lo,
    send, got, reply, back,
    row_send, row_got,
    acc, first, first_low, near_sum, dual_low, image,
    ag0, ag1, coeff, far_flat, far_in,
    asc_send, asc_got, asc_flat,
    tops, sums1, sums2,
    load_sem, send_sem, got_sem, row_send_sem, row_sem, reply_sem, back_sem,
    asc_send_sem, asc_sem, ag_send_sem, ag_sem, top_send_sem, top_sem, sum_send_sem, sum_sem,
):
    z, x, y, c = (lax.axis_index(a) for a in AXES)
    zs = [z] + [lax.rem(z + d, 4) for d in (1, 2, 3)]
    xs = [x] + [lax.rem(x + d, 4) for d in (1, 2, 3)]
    ys = [y] + [lax.rem(y + d, 4) for d in (1, 2, 3)]
    cs = [c, 1 - c]
    branch = z * 4 + x
    group = y * 2 + c
    me = branch * 8 + group

    loads = [
        pltpu.make_async_copy(src, dst, load_sem.at[n])
        for n, (src, dst) in enumerate(
            (
                (basis_hbm, basis), (gram_hbm, gram), (base_hbm, base), (asc_hbm, asc),
                (desc_hbm, desc), (far_hbm, far), (near_hbm, near),
            )
        )
    ]
    for load in loads:
        load.start()

    barrier = pltpu.get_barrier_semaphore()
    for k in range(1, DEV):
        pl.semaphore_signal(
            barrier, inc=1,
            device_id=(zs[k // 32], xs[k // 8 % 4], ys[k // 2 % 4], cs[k % 2]),
            device_id_type=MESH,
        )

    owners = lax.broadcasted_iota(jnp.int32, (DEV, ROWS), 0)
    hit0 = jnp.broadcast_to(owner_ref[0:1, :], (DEV, ROWS)) == owners
    hit1 = jnp.broadcast_to(owner_ref[1:2, :], (DEV, ROWS)) == owners
    hit = jnp.where(hit0, 1.0, 0.0) + jnp.where(hit1, 1.0, 0.0)
    weight = jnp.where(
        hit0, jnp.broadcast_to(weight_ref[0:1, :], (DEV, ROWS)),
        jnp.broadcast_to(weight_ref[1:2, :], (DEV, ROWS)),
    )
    high = weight.astype(BF16).astype(F32)
    weight_hi[...] = high
    weight_lo[...] = weight - high
    row_of[...] = jnp.where(
        hit0, jnp.broadcast_to(row_ref[0:1, :], (DEV, ROWS)),
        jnp.broadcast_to(row_ref[1:2, :], (DEV, ROWS)),
    ).astype(F32)
    upto = jnp.where(
        lax.broadcasted_iota(jnp.int32, (128, 128), 0) <= lax.broadcasted_iota(jnp.int32, (128, 128), 1),
        1.0, 0.0,
    ).astype(BF16)
    before = jnp.zeros((DEV, 1), F32)
    for n in range(ROWS // 128):
        part = hit[:, n * 128 : (n + 1) * 128]
        count = dot(part.astype(BF16), upto) + before
        rank_of[:, n * 128 : (n + 1) * 128] = jnp.where(part > 0.5, count - 1.0, -1.0)
        before = count[:, 127:128]

    loads[0].wait()
    vector = basis[1]
    vec_hi[...] = vector.astype(BF16)
    vec_lo[...] = (vector - vector.astype(BF16).astype(F32)).astype(BF16)

    pl.semaphore_wait(barrier, DEV - 1)

    def offsets(i):
        return lax.rem(i + 2, 4), lax.rem(i + 2 + i // 4, 4)

    def to_group(i):
        dz, dx = offsets(i)
        return lax.rem(z + dz, 4), lax.rem(x + dx, 4)

    def from_group(i):
        dz, dx = offsets(i)
        return lax.rem(z + 4 - dz, 4) * 4 + lax.rem(x + 4 - dx, 4)

    def remote(src, dst, send_s, recv_s, to):
        pltpu.make_async_remote_copy(
            src_ref=src, dst_ref=dst, send_sem=send_s, recv_sem=recv_s, device_id=to, device_id_type=MESH
        ).start()

    def wait_for(ref, sem):
        pltpu.make_async_copy(ref, ref, sem).wait()

    slot_at = lax.broadcasted_iota(jnp.int32, (SLOTS, ROWS), 0).astype(F32)
    lane_at = lax.broadcasted_iota(jnp.int32, (8, 128), 1)

    def spread_out(buf, into, s_sem, r_sem, i, tz, tx, tb):
        for dy in (2, 1, 3, 0):
            for dc in (1, 0):
                to = tb * 8 + ys[dy] * 2 + cs[dc]
                if dy == 0 and dc == 0:

                    @pl.when(i != SELF)
                    def _():
                        remote(buf.at[to], into.at[me], s_sem, r_sem.at[i], (tz, tx, ys[dy], cs[dc]))

                    @pl.when(i == SELF)
                    def _():
                        pltpu.make_async_copy(buf.at[me], into.at[me], r_sem.at[i]).start()
                else:
                    remote(buf.at[to], into.at[me], s_sem, r_sem.at[i], (tz, tx, ys[dy], cs[dc]))

    def fill(i, carry):
        tz, tx = to_group(i)
        tb = tz * 4 + tx
        eight = pl.ds(pl.multiple_of(tb * 8, 8), 8)
        ranks, w_hi, w_lo, rows = rank_of[eight, :], weight_hi[eight, :], weight_lo[eight, :], row_of[eight, :]
        listed = jnp.full((8, 128), -1.0, F32)
        for slot in range(SLOTS):
            found = jnp.max(jnp.where(ranks == float(slot), rows, -1.0), axis=1, keepdims=True)
            listed = jnp.where(lane_at == slot, jnp.broadcast_to(found, (8, 128)), listed)
        for o in range(8):
            row_send[tb * 8 + o] = listed[o : o + 1, :]
        spread_out(row_send, row_got, row_send_sem, row_sem, i, tz, tx, tb)
        for o in range(8):
            mask = jnp.broadcast_to(ranks[o : o + 1, :], (SLOTS, ROWS)) == slot_at
            pick_hi[tb * 8 + o] = jnp.where(mask, jnp.broadcast_to(w_hi[o : o + 1, :], (SLOTS, ROWS)), 0.0).astype(BF16)
            pick_lo[tb * 8 + o] = jnp.where(mask, jnp.broadcast_to(w_lo[o : o + 1, :], (SLOTS, ROWS)), 0.0).astype(BF16)
        g_hi = pick_hi[pl.ds(tb * 8, 8)].reshape(8 * SLOTS, ROWS)
        g_lo = pick_lo[pl.ds(tb * 8, 8)].reshape(8 * SLOTS, ROWS)
        values = dot(g_hi, vec_hi[...]) + (dot(g_hi, vec_lo[...]) + dot(g_lo, vec_hi[...]))
        send[pl.ds(tb * 8, 8)] = values.astype(BF16).reshape(8, SLOTS, COLS)
        spread_out(send, got, send_sem, got_sem, i, tz, tx, tb)
        return carry

    lax.fori_loop(0, 16, fill, 0)

    loads[3].wait()
    own = jnp.concatenate([asc[0], asc[1]], axis=1)
    asc_send[...] = own
    for k in range(1, 16):
        remote(asc_send, asc_got.at[branch], asc_send_sem, asc_sem, (zs[k // 4], xs[k % 4], y, c))
    asc_got[branch] = own

    v0, v1 = basis[0], basis[1]
    mutual = [jnp.sum(a * b, axis=0, keepdims=True) for a, b in ((v0, v0), (v0, v1), (v1, v1))]

    loads[5].wait()
    for leaf in range(2):
        for k in range(8):
            far_flat[leaf, :, k * 128 : (k + 1) * 128] = jnp.concatenate(
                [far[leaf, 2 * k], far[leaf, 2 * k + 1]], axis=1
            )

    acc[...] = jnp.zeros_like(acc)
    row_at = lax.broadcasted_iota(jnp.int32, (SLOTS, ROWS), 1).astype(F32)

    def gather(i, carry):
        sb = from_group(i)
        wait_for(row_got.at[pl.ds(0, 8)], row_sem.at[i])
        listed = jnp.concatenate([row_got[sb * 8 + o] for o in range(8)], axis=0)
        turned = jnp.transpose(listed)
        for o in range(8):
            rows = jnp.broadcast_to(turned[0:SLOTS, o : o + 1], (SLOTS, ROWS))
            place[sb * 8 + o] = jnp.where(rows == row_at, 1.0, 0.0).astype(BF16)
        wait_for(got.at[pl.ds(0, 8)], got_sem.at[i])
        chosen = place[pl.ds(sb * 8, 8)].reshape(8 * SLOTS, ROWS)
        acc[...] += dot_t(chosen, got[pl.ds(sb * 8, 8)].reshape(8 * SLOTS, COLS))
        return carry

    lax.fori_loop(0, 16, gather, 0)

    loads[1].wait()
    loads[2].wait()
    for leaf, (slots, i, j) in enumerate(((ag0, z, x), (ag1, x, z))):
        rows = pl.ds(leaf * LEAF, LEAF)
        dual = acc[rows, :]
        passed = dual + dot_t(gram[leaf], dual.astype(BF16))
        first[rows, :] = passed
        first_low[leaf] = passed.astype(BF16)
        slots[i, j] = dot(base[leaf], first_low[leaf]).astype(BF16)
    for d in (1, 3, 2):
        remote(ag0.at[z, x], ag0.at[z, x], ag_send_sem.at[0], ag_sem.at[0], (z, xs[d], y, c))
        remote(ag1.at[x, z], ag1.at[x, z], ag_send_sem.at[1], ag_sem.at[1], (zs[d], x, y, c))

    loads[6].wait()
    near_sum[...] = jnp.zeros_like(near_sum)

    def near_of(leaf):
        def step(k, carry):
            rows = pl.ds(leaf * LEAF, LEAF)
            near_sum[rows, :] += dot(near[leaf, k], first_low[near_list[leaf, k]])
            return carry

        lax.fori_loop(0, 8, step, 0)

    near_of(0)
    three = pl.ds(0, 3)
    wait_for(ag0.at[0, three], ag_sem.at[0])
    wait_for(ag1.at[0, three], ag_sem.at[1])
    for d in (1, 3, 2):
        remote(ag0.at[z], ag0.at[z], ag_send_sem.at[2], ag_sem.at[2], (zs[d], x, y, c))
        remote(ag1.at[x], ag1.at[x], ag_send_sem.at[3], ag_sem.at[3], (z, xs[d], y, c))
    near_of(1)
    wait_for(asc_got.at[pl.ds(0, 15)], asc_sem)
    for b in range(16):
        asc_flat[:, b * 128 : (b + 1) * 128] = asc_got[b]
    wait_for(ag0.at[three], ag_sem.at[2])
    wait_for(ag1.at[three], ag_sem.at[3])
    for b in range(16):
        coeff[2 * b] = ag0[b // 4, b % 4]
        coeff[2 * b + 1] = ag1[b % 4, b // 4]
    tops[group] = dot(asc_flat[...], coeff[...].reshape(32 * RANK, COLS)).astype(BF16)
    for k in range(1, 8):
        remote(tops.at[group], tops.at[group], top_send_sem, top_sem, (z, x, ys[k // 2], cs[k % 2]))
    for leaf in range(2):
        for k in range(16):
            far_in[leaf, k * RANK : (k + 1) * RANK, :] = coeff[far_list[leaf, k]]
    far_sum = [dot(far_flat[leaf], far_in[leaf]) for leaf in range(2)]
    loads[4].wait()
    wait_for(tops.at[pl.ds(0, 7)], top_sem)
    field = dot(top_ref[...], tops[...].reshape(8 * RANK, COLS)).astype(BF16)
    for leaf in range(2):
        rows = pl.ds(leaf * LEAF, LEAF)
        descent = (far_sum[leaf] + dot(desc[leaf], field)).astype(BF16)
        dual = first[rows, :] + near_sum[rows, :] + dot_t(base[leaf], descent)
        dual_low[rows, :] = (dual + dot(gram[leaf], dual.astype(BF16))).astype(BF16)

    def answer(i, carry):
        tz, tx = to_group(i)
        tb = tz * 4 + tx
        chosen = place[pl.ds(tb * 8, 8)].reshape(8 * SLOTS, ROWS)
        reply[pl.ds(tb * 8, 8)] = dot(chosen, dual_low[...]).astype(BF16).reshape(8, SLOTS, COLS)
        spread_out(reply, back, reply_sem, back_sem, i, tz, tx, tb)
        return carry

    lax.fori_loop(0, 16, answer, 0)

    image[...] = jnp.zeros_like(image)

    def collect(i, carry):
        sb = from_group(i)
        wait_for(back.at[pl.ds(0, 8)], back_sem.at[i])
        values = back[pl.ds(sb * 8, 8)].reshape(8 * SLOTS, COLS)
        g_hi = pick_hi[pl.ds(sb * 8, 8)].reshape(8 * SLOTS, ROWS)
        g_lo = pick_lo[pl.ds(sb * 8, 8)].reshape(8 * SLOTS, ROWS)
        image[...] += dot_t(g_hi, values) + dot_t(g_lo, values)
        return carry

    lax.fori_loop(0, 16, collect, 0)

    found = image[...]
    cross = [jnp.sum(basis[k] * found, axis=0, keepdims=True) for k in range(2)]
    whole = jnp.sum(found * found, axis=0, keepdims=True)
    sums1[group] = jnp.concatenate(cross + [whole] + mutual + [jnp.zeros((2, COLS), F32)], axis=0)
    for k in range(1, 8):
        remote(sums1.at[group], sums1.at[group], sum_send_sem.at[0], sum_sem.at[0], (z, x, ys[k // 2], cs[k % 2]))
    wait_for(sums1.at[pl.ds(0, 7)], sum_sem.at[0])
    sums2[branch] = jnp.sum(sums1[...], axis=0)
    for k in range(1, 16):
        remote(sums2.at[branch], sums2.at[branch], sum_send_sem.at[1], sum_sem.at[1], (zs[k // 4], xs[k % 4], y, c))
    wait_for(sums2.at[pl.ds(0, 15)], sum_sem.at[1])
    total = jnp.sum(sums2[...], axis=0) * (1.0 / TOTAL)
    p0, p1, sq = total[0:1], total[1:2], total[2:3]
    m00, m01, m11 = total[3:4], total[4:5], total[5:6]
    square = sq - 2.0 * (p0 * p0 + p1 * p1) + (p0 * p0 * m00 + 2.0 * (p0 * p1) * m01 + p1 * p1 * m11)
    norm = jnp.sqrt(square + 1e-6)
    hess_ref[...] = jnp.concatenate([p0, p1, norm], axis=0)
    scale = 1.0 / norm
    out_ref[...] = (image[...] - (p0 * basis[0] + p1 * basis[1])) * scale

    wait_for(row_send.at[pl.ds(0, DEV - 1)], row_send_sem)
    wait_for(send.at[pl.ds(0, DEV - 1)], send_sem)
    wait_for(reply.at[pl.ds(0, DEV - 1)], reply_sem)
    wait_for(asc_got.at[pl.ds(0, 15)], asc_send_sem)
    wait_for(ag0.at[0, three], ag_send_sem.at[0])
    wait_for(ag1.at[0, three], ag_send_sem.at[1])
    wait_for(ag0.at[three], ag_send_sem.at[2])
    wait_for(ag1.at[three], ag_send_sem.at[3])
    wait_for(tops.at[pl.ds(0, 7)], top_send_sem)
    wait_for(sums1.at[pl.ds(0, 7)], sum_send_sem.at[0])
    wait_for(sums2.at[pl.ds(0, 15)], sum_send_sem.at[1])


def body(
    basis, spread_owner, spread_row, spread_weight, gram_term, near_block, near_list,
    leaf_basis, far_block, far_list, ascend, descend, top_block,
):
    vmem = pl.BlockSpec(memory_space=pltpu.VMEM)
    smem = pl.BlockSpec(memory_space=pltpu.SMEM)
    hbm = pl.BlockSpec(memory_space=pl.ANY)
    dma = pltpu.SemaphoreType.DMA
    V = pltpu.VMEM
    return tuple(
        pl.pallas_call(
            kernel,
            out_shape=(
                jax.ShapeDtypeStruct((ROWS, COLS), F32),
                jax.ShapeDtypeStruct((3, COLS), F32),
            ),
            in_specs=[vmem] * 3 + [smem] * 2 + [vmem] + [hbm] * 7,
            out_specs=(vmem, vmem),
            scratch_shapes=[
                V((2, ROWS, COLS), F32), V((2, LEAF, LEAF), BF16), V((2, 8, LEAF, LEAF), BF16),
                V((2, RANK, LEAF), BF16), V((2, 16, RANK, RANK), BF16), V((2, RANK, RANK), BF16),
                V((2, RANK, RANK), BF16),
                V((DEV, ROWS), F32), V((DEV, ROWS), F32), V((DEV, ROWS), F32), V((DEV, ROWS), F32),
                V((DEV, SLOTS, ROWS), BF16), V((DEV, SLOTS, ROWS), BF16), V((DEV, SLOTS, ROWS), BF16),
                V((ROWS, COLS), BF16), V((ROWS, COLS), BF16),
                V((DEV, SLOTS, COLS), BF16), V((DEV, SLOTS, COLS), BF16),
                V((DEV, SLOTS, COLS), BF16), V((DEV, SLOTS, COLS), BF16),
                V((DEV, 1, 128), F32), V((DEV, 1, 128), F32),
                V((ROWS, COLS), F32), V((ROWS, COLS), F32), V((2, LEAF, COLS), BF16),
                V((ROWS, COLS), F32), V((ROWS, COLS), BF16), V((ROWS, COLS), F32),
                V((4, 4, RANK, COLS), BF16), V((4, 4, RANK, COLS), BF16), V((32, RANK, COLS), BF16),
                V((2, RANK, 16 * RANK), BF16), V((2, 16 * RANK, COLS), BF16),
                V((RANK, 2 * RANK), BF16), V((16, RANK, 2 * RANK), BF16), V((RANK, 32 * RANK), BF16),
                V((8, RANK, COLS), BF16), V((8, 8, COLS), F32), V((16, 8, COLS), F32),
                dma((7,)), dma, dma((16,)), dma, dma((16,)), dma, dma((16,)),
                dma, dma, dma((4,)), dma((4,)), dma, dma, dma((2,)), dma((2,)),
            ],
            compiler_params=pltpu.CompilerParams(
                collective_id=0, has_side_effects=True, vmem_limit_bytes=67_000_000
            ),
            name="dual_step",
        )(
            spread_owner.T, spread_row.T, spread_weight.T, near_list, far_list, top_block,
            basis, gram_term, near_block, leaf_basis, far_block, ascend, descend,
        )
    )


def solution(mesh):
    finer = Mesh(mesh.devices.reshape(4, 4, 4, 2), AXES)
    split = P(BRANCH_GROUP)
    return jax.shard_map(
        body,
        mesh=finer,
        in_specs=(
            P(None, BRANCH_GROUP, None), split, split, split, split, split, split,
            split, split, split, split, split, P(GROUP, None),
        ),
        out_specs=(P(BRANCH_GROUP, None), P()),
        check_vma=False,
    )
```

time: 336 us -> 113 us (0.34)
  waiting for transfers between devices: 116 us -> 0 us
  Pallas kernels: 0 us -> 109 us
  local copies, waits for them, and re-layouts: 64.1 us -> 3.53 us
  other arithmetic: 50.9 us -> 0 us
  blocking collectives: 47.2 us -> 0 us
  starting transfers between devices: 38.9 us -> 0 us
  matrix products: 15.8 us -> 0 us
    all_to_all x5 -> x0, waiting for transfers between devices: 116 us -> none  [the longest x1 52.4 us: body(): lax.all_to_all(replies.reshape(devices, slot_count, columns), BRANCH_GROU...]
    pallas_call x0 -> x1, Pallas kernels: none -> 109 us  [body(): pl.pallas_call(kernel, out_shape=(jax.ShapeDtypeStruct((ROWS, COLS), F32)...]
    all_to_all x5 -> x0, starting transfers between devices: 38.9 us -> none  [the longest x1 11.5 us: body(): lax.all_to_all(send_rows.reshape(devices, slot_count), BRANCH_GROUP, spli...]
    gather x5 -> x0, local copies, waits for them, and re-layouts: 35.1 us -> none  [the longest x1 16.1 us: body(): replies = dual_out[got_rows]]
    psum x4 -> x0, blocking collectives: 28.9 us -> none  [by_axis(): return functools.reduce(lax.psum, axes, shard)]
    scatter-add x1 -> x0, other arithmetic: 24 us -> none  [body(): dual_in = jnp.zeros((rows_dev, columns), jnp.float32).at[got_rows].add(go...]
    all_to_all x1 -> x0, blocking collectives: 18.4 us -> none  [copy_for_each(): return lax.all_to_all(copies, axis, split_axis=0, concat_axis=0, tiled=True)]
    dot_general x8 -> x0, matrix products: 15.8 us -> none  [the longest x7 14.2 us: contract(): jnp.einsum(pattern, first_op, second_op, preferred_element_type=jnp.float32)]
  transfers between devices with their start and end apart: 5 -> 0, of which waited for: 3 -> 0; matrix products, arithmetic and copies ran while one was open for 10% -> 0% of each run, Pallas kernels for 0% -> 0%
where the time goes in v1:
time: 113 us
  Pallas kernels  109 us (96%)
  local copies, waits for them, and re-layouts  3.53 us (3%)
    pallas_call x1, Pallas kernels, body(): pl.pallas_call(kernel, out_shape=(jax.ShapeDtypeStruct((ROWS, COLS), F32)...  109 us
    unnamed x2, local copies, waits for them, and re-layouts  3.53 us

profile of v1, /device:TPU:1, one launch (start us, length us, event | category | flops | bytes accessed | tf_op | source)
XLA Modules:
  0.0 113.0 jit_solution(7047176376084085260)
XLA Ops:
  0.6 108.8 %dual_step.1 = (f32[1024,256]{1,0:T(8,128)}, f32[3,256]{1,0:T(4,128)}) custom-call(s32[2,1024]{1,0:T(2,128)} %bitcast.3, s32[2,1024]{1,0:T(2,128)} %bitcast.4, f32[2,1024]{1,0:T(2,128)} %bitcast.5, s32[2,8]{1,0:T(2,128)} %near_list.1, s32[2,16]{1,0:T(2,128)} %far_list.1, bf16[64,512]{1,0:T(8,128)(2,1)} %top_ref.1, f32[2,1024,256]{2,1,0:T(8,128)} %basis_hbm.1, ...), custom_call_target="tpu_custom_call" | custom-call | tf_op jit(solution)/shard_map/dual_step/pallas_call | solution.py:332
  109.5 2.3 %copy.17 = f32[1024,256]{1,0:T(8,128)} copy(f32[1024,256]{1,0:T(8,128)} %get-tuple-element.4) | data formatting | bytes 2097152
  111.7 1.3 %copy.18 = f32[3,256]{1,0:T(4,128)} copy(f32[3,256]{1,0:T(4,128)} %get-tuple-element.5) | data formatting | bytes 6144

commit v2 on v1

v2 whole, which is shorter than its diff:
```python
import jax
import jax.numpy as jnp
from jax import lax
from jax.experimental import pallas as pl
from jax.experimental.pallas import tpu as pltpu
from jax.sharding import Mesh
from jax.sharding import PartitionSpec as P

AXES = ("branch_0", "branch_1", "group_0", "group_1")
BRANCH_GROUP = AXES
GROUP = AXES[2:]
MESH = pl.DeviceIdType.MESH
F32 = jnp.float32
BF16 = jnp.bfloat16
DEV = 128
SLOTS = 32
ROWS = 1024
LEAF = 512
RANK = 64
COLS = 256
TOTAL = DEV * ROWS
SELF = 2
PARTS = 2
WIDE = COLS // PARTS


def dot(a, b):
    return jnp.dot(a, b, preferred_element_type=F32)


def dot_t(a, b):
    return lax.dot_general(a, b, (((0,), (0,)), ((), ())), preferred_element_type=F32)


def kernel(
    owner_ref, row_ref, weight_ref, near_list, far_list, top_ref,
    basis_hbm, gram_hbm, near_hbm, base_hbm, far_hbm, asc_hbm, desc_hbm,
    image_hbm, total_ref,
    basis, gram, near, base, far, asc, desc,
    rank_of, rank_low, weight_of, row_of, count_of,
    pick, place, slot_weight, slot_low, vec,
    send, got, reply, back,
    row_send, row_got,
    acc, first, first_low, near_sum, dual_two, image, image_out,
    ag0, ag1, coeff, far_flat, far_in,
    par1, par2, tops, sums1, sums2,
    load_sem, send_sem, got_sem, row_send_sem, row_sem, reply_sem, back_sem,
    ag_send_sem, ag_sem, par_send_sem, par_sem, top_send_sem, top_sem, sum_send_sem, sum_sem, out_sem,
):
    z, x, y, c = (lax.axis_index(a) for a in AXES)
    zs = [z] + [lax.rem(z + d, 4) for d in (1, 2, 3)]
    xs = [x] + [lax.rem(x + d, 4) for d in (1, 2, 3)]
    ys = [y] + [lax.rem(y + d, 4) for d in (1, 2, 3)]
    cs = [c, 1 - c]
    branch = z * 4 + x
    group = y * 2 + c
    me = branch * 8 + group

    def remote(src, dst, send_s, recv_s, to):
        pltpu.make_async_remote_copy(
            src_ref=src, dst_ref=dst, send_sem=send_s, recv_sem=recv_s, device_id=to, device_id_type=MESH
        ).start()

    def wait_for(ref, sem):
        pltpu.make_async_copy(ref, ref, sem).wait()

    barrier = pltpu.get_barrier_semaphore()
    for k in range(1, DEV):
        pl.semaphore_signal(
            barrier, inc=1,
            device_id=(zs[k // 32], xs[k // 8 % 4], ys[k // 2 % 4], cs[k % 2]),
            device_id_type=MESH,
        )

    loads = [
        pltpu.make_async_copy(src, dst, load_sem.at[n])
        for n, (src, dst) in enumerate(
            (
                (basis_hbm.at[1], basis.at[1]), (basis_hbm.at[0], basis.at[0]), (gram_hbm, gram),
                (base_hbm, base), (asc_hbm, asc), (desc_hbm, desc), (far_hbm, far), (near_hbm, near),
            )
        )
    ]
    for load in loads:
        load.start()

    owners = lax.broadcasted_iota(jnp.int32, (DEV, ROWS), 0)
    hit0 = jnp.broadcast_to(owner_ref[0:1, :], (DEV, ROWS)) == owners
    hit1 = jnp.broadcast_to(owner_ref[1:2, :], (DEV, ROWS)) == owners
    hit = jnp.where(hit0, 1.0, 0.0) + jnp.where(hit1, 1.0, 0.0)
    weight_of[...] = jnp.where(
        hit0, jnp.broadcast_to(weight_ref[0:1, :], (DEV, ROWS)),
        jnp.broadcast_to(weight_ref[1:2, :], (DEV, ROWS)),
    )
    row_of[...] = jnp.where(
        hit0, jnp.broadcast_to(row_ref[0:1, :], (DEV, ROWS)),
        jnp.broadcast_to(row_ref[1:2, :], (DEV, ROWS)),
    ).astype(F32)
    upto = jnp.where(
        lax.broadcasted_iota(jnp.int32, (128, 128), 0) <= lax.broadcasted_iota(jnp.int32, (128, 128), 1),
        1.0, 0.0,
    ).astype(BF16)
    before = jnp.zeros((DEV, 1), F32)
    for n in range(ROWS // 128):
        part = hit[:, n * 128 : (n + 1) * 128]
        count = dot(part.astype(BF16), upto) + before
        rank_of[:, n * 128 : (n + 1) * 128] = jnp.where(part > 0.5, count - 1.0, -1.0)
        before = count[:, 127:128]
    count_of[...] = jnp.broadcast_to(before, (DEV, 128))
    rank_low[...] = jnp.where(rank_of[...] >= 0.0, rank_of[...] + jnp.broadcast_to(before, (DEV, ROWS)), -1.0)

    loads[0].wait()
    vector = basis[1]
    vec[:, 0:COLS] = vector.astype(BF16)
    vec[:, COLS:] = (vector - vector.astype(BF16).astype(F32)).astype(BF16)

    def offsets(i):
        return lax.rem(i + 2, 4), lax.rem(i + 2 + i // 4, 4)

    def to_group(i):
        dz, dx = offsets(i)
        return lax.rem(z + dz, 4), lax.rem(x + dx, 4)

    def from_group(i):
        dz, dx = offsets(i)
        return lax.rem(z + 4 - dz, 4) * 4 + lax.rem(x + 4 - dx, 4)

    def spread_out(buf, into, s_sem, r_sem, i):
        tz, tx = to_group(i)
        tb = tz * 4 + tx
        for dy in (2, 1, 3, 0):
            for dc in (1, 0):
                to = tb * 8 + ys[dy] * 2 + cs[dc]
                if dy == 0 and dc == 0:

                    @pl.when(i != SELF)
                    def _():
                        remote(buf.at[to], into.at[me], s_sem, r_sem.at[i], (tz, tx, ys[dy], cs[dc]))

                    @pl.when(i == SELF)
                    def _():
                        pltpu.make_async_copy(buf.at[me], into.at[me], r_sem.at[i]).start()
                else:
                    remote(buf.at[to], into.at[me], s_sem, r_sem.at[i], (tz, tx, ys[dy], cs[dc]))

    slot_at = lax.broadcasted_iota(jnp.int32, (SLOTS, ROWS), 0).astype(F32)
    slot_col = lax.broadcasted_iota(jnp.int32, (SLOTS, COLS), 0).astype(F32)
    lane_at = lax.broadcasted_iota(jnp.int32, (SLOTS, 128), 1)

    def fill(i, carry):
        tz, tx = to_group(i)
        tb = tz * 4 + tx
        eight = pl.ds(pl.multiple_of(tb * 8, 8), 8)
        ranks, lows, weights, rows = rank_of[eight, :], rank_low[eight, :], weight_of[eight, :], row_of[eight, :]
        counts = count_of[eight, :]
        listed = jnp.zeros((SLOTS, 128), F32)
        scales = []
        for o in range(8):
            mask = (jnp.broadcast_to(ranks[o : o + 1, :], (SLOTS, ROWS)) == slot_at) | (
                jnp.broadcast_to(lows[o : o + 1, :], (SLOTS, ROWS)) == slot_at
            )
            pick[tb * 8 + o] = jnp.where(mask, 1.0, 0.0).astype(BF16)
            scale = jnp.sum(
                jnp.where(mask, jnp.broadcast_to(weights[o : o + 1, :], (SLOTS, ROWS)), 0.0), axis=1, keepdims=True
            )
            row = jnp.sum(
                jnp.where(mask, jnp.broadcast_to(rows[o : o + 1, :], (SLOTS, ROWS)), 0.0), axis=1, keepdims=True
            )
            row = jnp.broadcast_to(row, (SLOTS, 128)) + jnp.where(
                slot_col[:, 0:128] >= jnp.broadcast_to(counts[o : o + 1, :], (SLOTS, 128)), float(ROWS), 0.0
            )
            listed = jnp.where(lane_at == o, row, listed)
            slot_weight[tb * 8 + o] = jnp.broadcast_to(scale, (SLOTS, 128))
            scales.append(jnp.broadcast_to(scale, (SLOTS, COLS)))
        turned = jnp.transpose(listed)
        for o in range(8):
            row_send[tb * 8 + o, :, 0:SLOTS] = turned[o : o + 1, :]

        values = dot(pick[pl.ds(tb * 8, 8)].reshape(8 * SLOTS, ROWS), vec[...])
        for o in range(8):
            part = values[o * SLOTS : (o + 1) * SLOTS, :]
            part = (part[:, 0:COLS] + part[:, COLS:]) * scales[o]
            high = part.astype(BF16).astype(F32)
            count = jnp.broadcast_to(counts[o : o + 1, 0:1], (SLOTS, COLS))
            sent = jnp.where(slot_col >= count, part - high, high).astype(BF16)
            for p in range(PARTS):
                send[p, tb * 8 + o] = sent[:, p * WIDE : (p + 1) * WIDE]

        @pl.when(i == 0)
        def _():
            pl.semaphore_wait(barrier, DEV - 1)

        spread_out(row_send, row_got, row_send_sem, row_sem, i)
        spread_out(send.at[0], got.at[0], send_sem.at[0], got_sem.at[0], i)
        return carry

    lax.fori_loop(0, 16, fill, 0)

    def fill_rest(i, carry):
        spread_out(send.at[1], got.at[1], send_sem.at[1], got_sem.at[1], i)
        return carry

    lax.fori_loop(0, 16, fill_rest, 0)

    loads[1].wait()
    v0, v1 = basis[0], basis[1]
    mutual = [jnp.sum(a * b, axis=0, keepdims=True) for a, b in ((v0, v0), (v0, v1), (v1, v1))]

    for n in range(2, 8):
        loads[n].wait()
    for leaf in range(2):
        for k in range(8):
            far_flat[leaf, :, k * 128 : (k + 1) * 128] = jnp.concatenate(
                [far[leaf, 2 * k], far[leaf, 2 * k + 1]], axis=1
            )

    acc[...] = jnp.zeros_like(acc)
    near_sum[...] = jnp.zeros_like(near_sum)
    image[...] = jnp.zeros_like(image)
    row_at = lax.broadcasted_iota(jnp.int32, (SLOTS, ROWS), 1).astype(F32)

    def find_places(i, carry):
        sb = from_group(i)
        wait_for(row_got.at[pl.ds(0, 8)], row_sem.at[i])
        turned = jnp.transpose(jnp.concatenate([row_got[sb * 8 + o] for o in range(8)], axis=0))
        for o in range(8):
            row = turned[0:SLOTS, o : o + 1]
            low = row >= float(ROWS)
            slot_low[sb * 8 + o] = jnp.broadcast_to(jnp.where(low, 1.0, 0.0), (SLOTS, 128))
            row = jnp.where(low, row - float(ROWS), row)
            place[sb * 8 + o] = jnp.where(jnp.broadcast_to(row, (SLOTS, ROWS)) == row_at, 1.0, 0.0).astype(BF16)
        return carry

    def gather(p, start, stop):
        def step(i, carry):
            sb = from_group(i)
            wait_for(got.at[p, pl.ds(0, 8)], got_sem.at[p, i])
            chosen = place[pl.ds(sb * 8, 8)].reshape(8 * SLOTS, ROWS)
            acc[p] += dot_t(chosen, got[p, pl.ds(sb * 8, 8)].reshape(8 * SLOTS, WIDE))
            return carry

        lax.fori_loop(start, stop, step, 0)

    half = RANK // 2

    def early(p):
        partial = jnp.zeros((RANK, WIDE), F32)
        for leaf, (slots, i, j) in enumerate(((ag0, z, x), (ag1, x, z))):
            rows = pl.ds(leaf * LEAF, LEAF)
            dual = acc[p, rows, :]
            passed = dual + dot_t(gram[leaf], dual.astype(BF16))
            first[p, rows, :] = passed
            first_low[p, leaf] = passed.astype(BF16)
            low = dot(base[leaf], first_low[p, leaf]).astype(BF16)
            slots[p, i, j] = low
            partial = partial + dot(asc[leaf], low)
        par1[p, 0, x] = partial[0:half].astype(BF16)
        par1[p, 1, z] = partial[half:].astype(BF16)
        for d in (1, 3, 2):
            remote(par1.at[p, 0, x], par1.at[p, 0, x], par_send_sem.at[p, 0], par_sem.at[p, 0], (z, xs[d], y, c))
            remote(par1.at[p, 1, z], par1.at[p, 1, z], par_send_sem.at[p, 1], par_sem.at[p, 1], (zs[d], x, y, c))
        for d in (1, 3, 2):
            remote(ag0.at[p, z, x], ag0.at[p, z, x], ag_send_sem.at[p, 0], ag_sem.at[p, 0], (z, xs[d], y, c))
            remote(ag1.at[p, x, z], ag1.at[p, x, z], ag_send_sem.at[p, 1], ag_sem.at[p, 1], (zs[d], x, y, c))

    def near_of(p, leaf):
        def step(k, carry):
            rows = pl.ds(leaf * LEAF, LEAF)
            near_sum[p, rows, :] += dot(near[leaf, k], first_low[p, near_list[leaf, k]])
            return carry

        lax.fori_loop(0, 8, step, 0)

    three = pl.ds(0, 3)

    def summed(ref):
        return ((ref[0].astype(F32) + ref[1].astype(F32)) + (ref[2].astype(F32) + ref[3].astype(F32))).astype(BF16)

    def mid_a(p):
        wait_for(par1.at[p, 0, three], par_sem.at[p, 0])
        wait_for(par1.at[p, 1, three], par_sem.at[p, 1])
        par2[p, 0, z] = summed(par1.at[p, 0])
        par2[p, 1, x] = summed(par1.at[p, 1])
        for d in (1, 3, 2):
            remote(par2.at[p, 0, z], par2.at[p, 0, z], par_send_sem.at[p, 2], par_sem.at[p, 2], (zs[d], x, y, c))
            remote(par2.at[p, 1, x], par2.at[p, 1, x], par_send_sem.at[p, 3], par_sem.at[p, 3], (z, xs[d], y, c))
        wait_for(ag0.at[p, 0, three], ag_sem.at[p, 0])
        wait_for(ag1.at[p, 0, three], ag_sem.at[p, 1])
        for d in (1, 3, 2):
            remote(ag0.at[p, z], ag0.at[p, z], ag_send_sem.at[p, 2], ag_sem.at[p, 2], (zs[d], x, y, c))
            remote(ag1.at[p, x], ag1.at[p, x], ag_send_sem.at[p, 3], ag_sem.at[p, 3], (z, xs[d], y, c))

    def mid_b(p):
        wait_for(par2.at[p, 0, three], par_sem.at[p, 2])
        wait_for(par2.at[p, 1, three], par_sem.at[p, 3])
        tops[p, group, 0:half] = summed(par2.at[p, 0])
        tops[p, group, half:] = summed(par2.at[p, 1])
        for k in range(1, 8):
            remote(tops.at[p, group], tops.at[p, group], top_send_sem.at[p], top_sem.at[p], (z, x, ys[k // 2], cs[k % 2]))

    def mid_c(p):
        wait_for(tops.at[p, pl.ds(0, 7)], top_sem.at[p])
        field = dot(top_ref[...], tops[p].reshape(8 * RANK, WIDE)).astype(BF16)
        wait_for(ag0.at[p, three], ag_sem.at[p, 2])
        wait_for(ag1.at[p, three], ag_sem.at[p, 3])
        for b in range(16):
            coeff[2 * b] = ag0[p, b // 4, b % 4]
            coeff[2 * b + 1] = ag1[p, b % 4, b // 4]
        for leaf in range(2):
            for k in range(16):
                far_in[k * RANK : (k + 1) * RANK, :] = coeff[far_list[leaf, k]]
            rows = pl.ds(leaf * LEAF, LEAF)
            descent = (dot(far_flat[leaf], far_in[...]) + dot(desc[leaf], field)).astype(BF16)
            dual = first[p, rows, :] + near_sum[p, rows, :] + dot_t(base[leaf], descent)
            dual = dual + dot(gram[leaf], dual.astype(BF16))
            dual_two[p, rows, 0:WIDE] = dual.astype(BF16)
            dual_two[p, rows, WIDE:] = (dual - dual.astype(BF16).astype(F32)).astype(BF16)

    def answer(p, start, stop):
        def step(i, carry):
            tz, tx = to_group(i)
            eight = pl.ds((tz * 4 + tx) * 8, 8)
            both = dot(place[eight].reshape(8 * SLOTS, ROWS), dual_two[p])
            low = slot_low[eight].reshape(8 * SLOTS, 128) > 0.5
            reply[p, eight] = jnp.where(low, both[:, WIDE:], both[:, 0:WIDE]).astype(BF16).reshape(8, SLOTS, WIDE)
            spread_out(reply.at[p], back.at[p], reply_sem.at[p], back_sem.at[p], i)
            return carry

        lax.fori_loop(start, stop, step, 0)

    def collect(p):
        def step(i, carry):
            eight = pl.ds(from_group(i) * 8, 8)
            wait_for(back.at[p, pl.ds(0, 8)], back_sem.at[p, i])
            values = back[p, eight].reshape(8 * SLOTS, WIDE).astype(F32) * slot_weight[eight].reshape(8 * SLOTS, 128)
            high = values.astype(BF16)
            two = jnp.concatenate([high, (values - high.astype(F32)).astype(BF16)], axis=1)
            both = dot_t(pick[eight].reshape(8 * SLOTS, ROWS), two)
            image[p] += both[:, 0:WIDE] + both[:, WIDE:]
            return carry

        lax.fori_loop(0, 16, step, 0)

    lax.fori_loop(0, 16, find_places, 0)
    gather(0, 0, 16)
    early(0)
    near_of(0, 0)
    near_of(0, 1)
    gather(1, 0, 12)
    mid_a(0)
    gather(1, 12, 16)
    early(1)
    mid_b(0)
    near_of(1, 0)
    mid_a(1)
    mid_c(0)
    answer(0, 0, 8)
    mid_b(1)
    answer(0, 8, 16)
    near_of(1, 1)
    mid_c(1)
    answer(1, 0, 16)
    collect(0)
    collect(1)

    found = jnp.concatenate([image[0], image[1]], axis=1)
    image_out[...] = found
    cross = [jnp.sum(basis[k] * found, axis=0, keepdims=True) for k in range(2)]
    whole = jnp.sum(found * found, axis=0, keepdims=True)
    sums1[group] = jnp.concatenate(cross + [whole] + mutual + [jnp.zeros((2, COLS), F32)], axis=0)
    for k in range(1, 8):
        remote(sums1.at[group], sums1.at[group], sum_send_sem.at[0], sum_sem.at[0], (z, x, ys[k // 2], cs[k % 2]))
    leave = pltpu.make_async_copy(image_out, image_hbm, out_sem)
    leave.start()
    wait_for(sums1.at[pl.ds(0, 7)], sum_sem.at[0])
    sums2[branch] = jnp.sum(sums1[...], axis=0)
    for k in range(1, 16):
        remote(sums2.at[branch], sums2.at[branch], sum_send_sem.at[1], sum_sem.at[1], (zs[k // 4], xs[k % 4], y, c))
    wait_for(row_send.at[pl.ds(0, DEV - 1)], row_send_sem)
    for p in range(PARTS):
        wait_for(send.at[p, pl.ds(0, DEV - 1)], send_sem.at[p])
        wait_for(reply.at[p, pl.ds(0, DEV - 1)], reply_sem.at[p])
        wait_for(ag0.at[p, 0, three], ag_send_sem.at[p, 0])
        wait_for(ag1.at[p, 0, three], ag_send_sem.at[p, 1])
        wait_for(ag0.at[p, three], ag_send_sem.at[p, 2])
        wait_for(ag1.at[p, three], ag_send_sem.at[p, 3])
        for n in range(4):
            wait_for(par1.at[p, 0, three], par_send_sem.at[p, n])
        wait_for(tops.at[p, pl.ds(0, 7)], top_send_sem.at[p])
    leave.wait()
    wait_for(sums1.at[pl.ds(0, 7)], sum_send_sem.at[0])
    wait_for(sums2.at[pl.ds(0, 15)], sum_sem.at[1])
    wait_for(sums2.at[pl.ds(0, 15)], sum_send_sem.at[1])
    total = jnp.sum(sums2[...], axis=0) * (1.0 / TOTAL)
    p0, p1, sq = total[0:1], total[1:2], total[2:3]
    m00, m01, m11 = total[3:4], total[4:5], total[5:6]
    square = sq - 2.0 * (p0 * p0 + p1 * p1) + (p0 * p0 * m00 + 2.0 * (p0 * p1) * m01 + p1 * p1 * m11)
    norm = jnp.sqrt(square + 1e-6)
    total_ref[...] = jnp.concatenate([p0, p1, norm, 1.0 / norm, jnp.zeros((4, COLS), F32)], axis=0)


def finish(total_ref, basis_ref, image_ref, out_ref, hess_ref):
    p0, p1, scale = total_ref[0:1], total_ref[1:2], total_ref[3:4]
    out_ref[...] = (image_ref[...] - (p0 * basis_ref[0] + p1 * basis_ref[1])) * scale
    hess_ref[...] = total_ref[0:3]


def body(
    basis, spread_owner, spread_row, spread_weight, gram_term, near_block, near_list,
    leaf_basis, far_block, far_list, ascend, descend, top_block,
):
    vmem = pl.BlockSpec(memory_space=pltpu.VMEM)
    smem = pl.BlockSpec(memory_space=pltpu.SMEM)
    hbm = pl.BlockSpec(memory_space=pl.ANY)
    dma = pltpu.SemaphoreType.DMA
    V = pltpu.VMEM
    image, total = pl.pallas_call(
        kernel,
        out_shape=(
            jax.ShapeDtypeStruct((ROWS, COLS), F32),
            jax.ShapeDtypeStruct((8, COLS), F32),
        ),
        in_specs=[vmem] * 3 + [smem] * 2 + [vmem] + [hbm] * 7,
        out_specs=(hbm, vmem),
        scratch_shapes=[
            V((2, ROWS, COLS), F32), V((2, LEAF, LEAF), BF16), V((2, 8, LEAF, LEAF), BF16),
            V((2, RANK, LEAF), BF16), V((2, 16, RANK, RANK), BF16), V((2, RANK, RANK), BF16),
            V((2, RANK, RANK), BF16),
            V((DEV, ROWS), F32), V((DEV, ROWS), F32), V((DEV, ROWS), F32), V((DEV, ROWS), F32), V((DEV, 128), F32),
            V((DEV, SLOTS, ROWS), BF16), V((DEV, SLOTS, ROWS), BF16),
            V((DEV, SLOTS, 128), F32), V((DEV, SLOTS, 128), F32), V((ROWS, 2 * COLS), BF16),
            V((PARTS, DEV, SLOTS, WIDE), BF16), V((PARTS, DEV, SLOTS, WIDE), BF16),
            V((PARTS, DEV, SLOTS, WIDE), BF16), V((PARTS, DEV, SLOTS, WIDE), BF16),
            V((DEV, 1, 128), F32), V((DEV, 1, 128), F32),
            V((PARTS, ROWS, WIDE), F32), V((PARTS, ROWS, WIDE), F32), V((PARTS, 2, LEAF, WIDE), BF16),
            V((PARTS, ROWS, WIDE), F32), V((PARTS, ROWS, 2 * WIDE), BF16), V((PARTS, ROWS, WIDE), F32),
            V((ROWS, COLS), F32),
            V((PARTS, 4, 4, RANK, WIDE), BF16), V((PARTS, 4, 4, RANK, WIDE), BF16), V((32, RANK, WIDE), BF16),
            V((2, RANK, 16 * RANK), BF16), V((16 * RANK, WIDE), BF16),
            V((PARTS, 2, 4, RANK // 2, WIDE), BF16), V((PARTS, 2, 4, RANK // 2, WIDE), BF16),
            V((PARTS, 8, RANK, WIDE), BF16), V((8, 8, COLS), F32), V((16, 8, COLS), F32),
            dma((8,)), dma((PARTS,)), dma((PARTS, 16)), dma, dma((16,)), dma((PARTS,)), dma((PARTS, 16)),
            dma((PARTS, 4)), dma((PARTS, 4)), dma((PARTS, 4)), dma((PARTS, 4)), dma((PARTS,)), dma((PARTS,)),
            dma((2,)), dma((2,)), dma,
        ],
        compiler_params=pltpu.CompilerParams(
            collective_id=0, has_side_effects=True, vmem_limit_bytes=67_000_000
        ),
        name="dual_step",
    )(
        spread_owner.T, spread_row.T, spread_weight.T, near_list, far_list, top_block,
        basis, gram_term, near_block, leaf_basis, far_block, ascend, descend,
    )
    rows = ROWS // 4
    return tuple(
        pl.pallas_call(
            finish,
            grid=(4,),
            out_shape=(jax.ShapeDtypeStruct((ROWS, COLS), F32), jax.ShapeDtypeStruct((3, COLS), F32)),
            in_specs=[
                pl.BlockSpec((8, COLS), lambda i: (0, 0)),
                pl.BlockSpec((2, rows, COLS), lambda i: (0, i, 0)),
                pl.BlockSpec((rows, COLS), lambda i: (i, 0)),
            ],
            out_specs=(pl.BlockSpec((rows, COLS), lambda i: (i, 0)), pl.BlockSpec((3, COLS), lambda i: (0, 0))),
            name="finish",
        )(total, basis, image)
    )


def solution(mesh):
    finer = Mesh(mesh.devices.reshape(4, 4, 4, 2), AXES)
    split = P(BRANCH_GROUP)
    return jax.shard_map(
        body,
        mesh=finer,
        in_specs=(
            P(None, BRANCH_GROUP, None), split, split, split, split, split, split,
            split, split, split, split, split, P(GROUP, None),
        ),
        out_specs=(P(BRANCH_GROUP, None), P()),
        check_vma=False,
    )
```

time: 113 us -> 103 us (0.912)
  Pallas kernels: 109 us -> 102 us
  local copies, waits for them, and re-layouts: 3.53 us -> 0 us
    pallas_call x1, Pallas kernels: 109 us -> 98.4 us  [body(): pl.pallas_call(kernel, out_shape=(jax.ShapeDtypeStruct((ROWS, COLS), F32)...]
    pallas_call x0 -> x1, Pallas kernels: none -> 3.8 us  [body(): pl.pallas_call(finish, grid=(4,), out_shape=(jax.ShapeDtypeStruct((ROWS,...]
    unnamed x2 -> x0, local copies, waits for them, and re-layouts: 3.53 us -> none
where the time goes in v2:
time: 103 us
  Pallas kernels  102 us (99%)
    pallas_call x1, Pallas kernels, body(): pl.pallas_call(kernel, out_shape=(jax.ShapeDtypeStruct((ROWS, COLS), F32)...  98.4 us
    pallas_call x1, Pallas kernels, body(): pl.pallas_call(finish, grid=(4,), out_shape=(jax.ShapeDtypeStruct((ROWS,...  3.8 us

profile of v2, /device:TPU:1, one launch (start us, length us, event | category | flops | bytes accessed | tf_op | source)
XLA Modules:
  0.0 102.9 jit_solution(5295870663357929487)
XLA Ops:
  0.6 98.4 %dual_step.1 = (f32[1024,256]{1,0:T(8,128)}, f32[8,256]{1,0:T(8,128)}) custom-call(s32[2,1024]{1,0:T(2,128)} %bitcast.3, s32[2,1024]{1,0:T(2,128)} %bitcast.4, f32[2,1024]{1,0:T(2,128)} %bitcast.5, s32[2,8]{1,0:T(2,128)} %near_list.1, s32[2,16]{1,0:T(2,128)} %far_list.1, bf16[64,512]{1,0:T(8,128)(2,1)} %top_ref.1, f32[2,1024,256]{2,1,0:T(8,128)} %basis_ref.1, ...), custom_call_target="tpu_custom_call" | custom-call | tf_op jit(solution)/shard_map/dual_step/pallas_call | solution.py:417
  99.1 3.8 %finish.1 = (f32[1024,256]{1,0:T(8,128)}, f32[3,256]{1,0:T(4,128)}) custom-call(f32[8,256]{1,0:T(8,128)} %get-tuple-element.4.total_ref, f32[2,1024,256]{2,1,0:T(8,128)} %basis_ref.1, f32[1024,256]{1,0:T(8,128)} %get-tuple-element.5.image_ref), custom_call_target="tpu_custom_call" | custom-call | tf_op jit(solution)/shard_map/finish/pallas_call | solution.py:456

commit v3 on v2

--- a/solution.py
+++ b/solution.py
@@ -20,6 +20,7 @@
 COLS = 256
 TOTAL = DEV * ROWS
 SELF = 2
+HELD = 12
 PARTS = 2
 WIDE = COLS // PARTS
 
@@ -123,25 +124,24 @@
 
     def from_group(i):
         dz, dx = offsets(i)
-        return lax.rem(z + 4 - dz, 4) * 4 + lax.rem(x + 4 - dx, 4)
-
-    def spread_out(buf, into, s_sem, r_sem, i):
-        tz, tx = to_group(i)
-        tb = tz * 4 + tx
+        return lax.rem(z + 4 - dz, 4), lax.rem(x + 4 - dx, 4)
+
+    def spread_out(buf, into, s_sem, r_sem, i, tz, tx):
+        mine = i * 8 + group
         for dy in (2, 1, 3, 0):
             for dc in (1, 0):
-                to = tb * 8 + ys[dy] * 2 + cs[dc]
+                src = buf.at[i * 8 + ys[dy] * 2 + cs[dc]]
                 if dy == 0 and dc == 0:
 
                     @pl.when(i != SELF)
                     def _():
-                        remote(buf.at[to], into.at[me], s_sem, r_sem.at[i], (tz, tx, ys[dy], cs[dc]))
+                        remote(src, into.at[mine], s_sem, r_sem.at[i], (tz, tx, ys[dy], cs[dc]))
 
                     @pl.when(i == SELF)
                     def _():
-                        pltpu.make_async_copy(buf.at[me], into.at[me], r_sem.at[i]).start()
+                        pltpu.make_async_copy(src, into.at[mine], r_sem.at[i]).start()
                 else:
-                    remote(buf.at[to], into.at[me], s_sem, r_sem.at[i], (tz, tx, ys[dy], cs[dc]))
+                    remote(src, into.at[mine], s_sem, r_sem.at[i], (tz, tx, ys[dy], cs[dc]))
 
     slot_at = lax.broadcasted_iota(jnp.int32, (SLOTS, ROWS), 0).astype(F32)
     slot_col = lax.broadcasted_iota(jnp.int32, (SLOTS, COLS), 0).astype(F32)
@@ -149,8 +149,7 @@
 
     def fill(i, carry):
         tz, tx = to_group(i)
-        tb = tz * 4 + tx
-        eight = pl.ds(pl.multiple_of(tb * 8, 8), 8)
+        eight = pl.ds(pl.multiple_of((tz * 4 + tx) * 8, 8), 8)
         ranks, lows, weights, rows = rank_of[eight, :], rank_low[eight, :], weight_of[eight, :], row_of[eight, :]
         counts = count_of[eight, :]
         listed = jnp.zeros((SLOTS, 128), F32)
@@ -159,7 +158,7 @@
             mask = (jnp.broadcast_to(ranks[o : o + 1, :], (SLOTS, ROWS)) == slot_at) | (
                 jnp.broadcast_to(lows[o : o + 1, :], (SLOTS, ROWS)) == slot_at
             )
-            pick[tb * 8 + o] = jnp.where(mask, 1.0, 0.0).astype(BF16)
+            pick[i * 8 + o] = jnp.where(mask, 1.0, 0.0).astype(BF16)
             scale = jnp.sum(
                 jnp.where(mask, jnp.broadcast_to(weights[o : o + 1, :], (SLOTS, ROWS)), 0.0), axis=1, keepdims=True
             )
@@ -170,13 +169,13 @@
                 slot_col[:, 0:128] >= jnp.broadcast_to(counts[o : o + 1, :], (SLOTS, 128)), float(ROWS), 0.0
             )
             listed = jnp.where(lane_at == o, row, listed)
-            slot_weight[tb * 8 + o] = jnp.broadcast_to(scale, (SLOTS, 128))
+            slot_weight[i * 8 + o] = jnp.broadcast_to(scale, (SLOTS, 128))
             scales.append(jnp.broadcast_to(scale, (SLOTS, COLS)))
         turned = jnp.transpose(listed)
         for o in range(8):
-            row_send[tb * 8 + o, :, 0:SLOTS] = turned[o : o + 1, :]
-
-        values = dot(pick[pl.ds(tb * 8, 8)].reshape(8 * SLOTS, ROWS), vec[...])
+            row_send[i * 8 + o, :, 0:SLOTS] = turned[o : o + 1, :]
+
+        values = dot(pick[pl.ds(i * 8, 8)].reshape(8 * SLOTS, ROWS), vec[...])
         for o in range(8):
             part = values[o * SLOTS : (o + 1) * SLOTS, :]
             part = (part[:, 0:COLS] + part[:, COLS:]) * scales[o]
@@ -184,62 +183,51 @@
             count = jnp.broadcast_to(counts[o : o + 1, 0:1], (SLOTS, COLS))
             sent = jnp.where(slot_col >= count, part - high, high).astype(BF16)
             for p in range(PARTS):
-                send[p, tb * 8 + o] = sent[:, p * WIDE : (p + 1) * WIDE]
+                send[p, i * 8 + o] = sent[:, p * WIDE : (p + 1) * WIDE]
 
         @pl.when(i == 0)
         def _():
             pl.semaphore_wait(barrier, DEV - 1)
 
-        spread_out(row_send, row_got, row_send_sem, row_sem, i)
-        spread_out(send.at[0], got.at[0], send_sem.at[0], got_sem.at[0], i)
+        spread_out(row_send, row_got, row_send_sem, row_sem, i, tz, tx)
+        spread_out(send.at[0], got.at[0], send_sem.at[0], got_sem.at[0], i, tz, tx)
         return carry
 
     lax.fori_loop(0, 16, fill, 0)
 
     def fill_rest(i, carry):
-        spread_out(send.at[1], got.at[1], send_sem.at[1], got_sem.at[1], i)
+        spread_out(send.at[1], got.at[1], send_sem.at[1], got_sem.at[1], i, *to_group(i))
         return carry
-
-    lax.fori_loop(0, 16, fill_rest, 0)
-
-    loads[1].wait()
-    v0, v1 = basis[0], basis[1]
-    mutual = [jnp.sum(a * b, axis=0, keepdims=True) for a, b in ((v0, v0), (v0, v1), (v1, v1))]
 
     for n in range(2, 8):
         loads[n].wait()
-    for leaf in range(2):
-        for k in range(8):
-            far_flat[leaf, :, k * 128 : (k + 1) * 128] = jnp.concatenate(
-                [far[leaf, 2 * k], far[leaf, 2 * k + 1]], axis=1
-            )
-
     acc[...] = jnp.zeros_like(acc)
-    near_sum[...] = jnp.zeros_like(near_sum)
     image[...] = jnp.zeros_like(image)
     row_at = lax.broadcasted_iota(jnp.int32, (SLOTS, ROWS), 1).astype(F32)
 
     def find_places(i, carry):
-        sb = from_group(i)
         wait_for(row_got.at[pl.ds(0, 8)], row_sem.at[i])
-        turned = jnp.transpose(jnp.concatenate([row_got[sb * 8 + o] for o in range(8)], axis=0))
+        turned = jnp.transpose(jnp.concatenate([row_got[i * 8 + o] for o in range(8)], axis=0))
         for o in range(8):
             row = turned[0:SLOTS, o : o + 1]
             low = row >= float(ROWS)
-            slot_low[sb * 8 + o] = jnp.broadcast_to(jnp.where(low, 1.0, 0.0), (SLOTS, 128))
+            slot_low[i * 8 + o] = jnp.broadcast_to(jnp.where(low, 1.0, 0.0), (SLOTS, 128))
             row = jnp.where(low, row - float(ROWS), row)
-            place[sb * 8 + o] = jnp.where(jnp.broadcast_to(row, (SLOTS, ROWS)) == row_at, 1.0, 0.0).astype(BF16)
+            place[i * 8 + o] = jnp.where(jnp.broadcast_to(row, (SLOTS, ROWS)) == row_at, 1.0, 0.0).astype(BF16)
         return carry
 
+    def four(q):
+        return pl.ds(pl.multiple_of(q * 32, 32), 32)
+
     def gather(p, start, stop):
-        def step(i, carry):
-            sb = from_group(i)
-            wait_for(got.at[p, pl.ds(0, 8)], got_sem.at[p, i])
-            chosen = place[pl.ds(sb * 8, 8)].reshape(8 * SLOTS, ROWS)
-            acc[p] += dot_t(chosen, got[p, pl.ds(sb * 8, 8)].reshape(8 * SLOTS, WIDE))
+        def step(q, carry):
+            for n in range(4):
+                wait_for(got.at[p, pl.ds(0, 8)], got_sem.at[p, q * 4 + n])
+            chosen = place[four(q)].reshape(32 * SLOTS, ROWS)
+            acc[p] += dot_t(chosen, got[p, four(q)].reshape(32 * SLOTS, WIDE))
             return carry
 
-        lax.fori_loop(start, stop, step, 0)
+        lax.fori_loop(start // 4, stop // 4, step, 0)
 
     half = RANK // 2
 
@@ -264,12 +252,10 @@
             remote(ag1.at[p, x, z], ag1.at[p, x, z], ag_send_sem.at[p, 1], ag_sem.at[p, 1], (zs[d], x, y, c))
 
     def near_of(p, leaf):
-        def step(k, carry):
-            rows = pl.ds(leaf * LEAF, LEAF)
-            near_sum[p, rows, :] += dot(near[leaf, k], first_low[p, near_list[leaf, k]])
-            return carry
-
-        lax.fori_loop(0, 8, step, 0)
+        found = dot(near[leaf, 0], first_low[p, near_list[leaf, 0]])
+        for k in range(1, 8):
+            found = found + dot(near[leaf, k], first_low[p, near_list[leaf, k]])
+        near_sum[p, pl.ds(leaf * LEAF, LEAF), :] = found
 
     three = pl.ds(0, 3)
 
@@ -317,38 +303,48 @@
             dual_two[p, rows, WIDE:] = (dual - dual.astype(BF16).astype(F32)).astype(BF16)
 
     def answer(p, start, stop):
-        def step(i, carry):
-            tz, tx = to_group(i)
-            eight = pl.ds((tz * 4 + tx) * 8, 8)
-            both = dot(place[eight].reshape(8 * SLOTS, ROWS), dual_two[p])
-            low = slot_low[eight].reshape(8 * SLOTS, 128) > 0.5
-            reply[p, eight] = jnp.where(low, both[:, WIDE:], both[:, 0:WIDE]).astype(BF16).reshape(8, SLOTS, WIDE)
-            spread_out(reply.at[p], back.at[p], reply_sem.at[p], back_sem.at[p], i)
+        def step(q, carry):
+            both = dot(place[four(q)].reshape(32 * SLOTS, ROWS), dual_two[p])
+            low = slot_low[four(q)].reshape(32 * SLOTS, 128) > 0.5
+            reply[p, four(q)] = jnp.where(low, both[:, WIDE:], both[:, 0:WIDE]).astype(BF16).reshape(32, SLOTS, WIDE)
+            for n in range(4):
+                i = q * 4 + n
+                spread_out(reply.at[p], back.at[p], reply_sem.at[p], back_sem.at[p], i, *from_group(i))
             return carry
 
-        lax.fori_loop(start, stop, step, 0)
+        lax.fori_loop(start // 4, stop // 4, step, 0)
 
     def collect(p):
-        def step(i, carry):
-            eight = pl.ds(from_group(i) * 8, 8)
-            wait_for(back.at[p, pl.ds(0, 8)], back_sem.at[p, i])
-            values = back[p, eight].reshape(8 * SLOTS, WIDE).astype(F32) * slot_weight[eight].reshape(8 * SLOTS, 128)
+        def step(q, carry):
+            for n in range(4):
+                wait_for(back.at[p, pl.ds(0, 8)], back_sem.at[p, q * 4 + n])
+            values = back[p, four(q)].reshape(32 * SLOTS, WIDE).astype(F32) * slot_weight[four(q)].reshape(32 * SLOTS, 128)
             high = values.astype(BF16)
             two = jnp.concatenate([high, (values - high.astype(F32)).astype(BF16)], axis=1)
-            both = dot_t(pick[eight].reshape(8 * SLOTS, ROWS), two)
+            both = dot_t(pick[four(q)].reshape(32 * SLOTS, ROWS), two)
             image[p] += both[:, 0:WIDE] + both[:, WIDE:]
             return carry
 
-        lax.fori_loop(0, 16, step, 0)
-
+        lax.fori_loop(0, 4, step, 0)
+
+    def flatten_far():
+        for leaf in range(2):
+            for k in range(8):
+                far_flat[leaf, :, k * 128 : (k + 1) * 128] = jnp.concatenate(
+                    [far[leaf, 2 * k], far[leaf, 2 * k + 1]], axis=1
+                )
+
+    lax.fori_loop(0, HELD, fill_rest, 0)
     lax.fori_loop(0, 16, find_places, 0)
+    flatten_far()
     gather(0, 0, 16)
     early(0)
+    lax.fori_loop(HELD, 16, fill_rest, 0)
     near_of(0, 0)
     near_of(0, 1)
-    gather(1, 0, 12)
+    gather(1, 0, 8)
     mid_a(0)
-    gather(1, 12, 16)
+    gather(1, 8, 16)
     early(1)
     mid_b(0)
     near_of(1, 0)
@@ -360,6 +356,9 @@
     near_of(1, 1)
     mid_c(1)
     answer(1, 0, 16)
+    loads[1].wait()
+    v0, v1 = basis[0], basis[1]
+    mutual = [jnp.sum(a * b, axis=0, keepdims=True) for a, b in ((v0, v0), (v0, v1), (v1, v1))]
     collect(0)
     collect(1)
 

time: 103 us -> 96.1 us (0.933)
  Pallas kernels: 102 us -> 95.2 us
    pallas_call x1, Pallas kernels: 98.4 us -> 91.4 us  [body(): pl.pallas_call(kernel, out_shape=(jax.ShapeDtypeStruct((ROWS, COLS), F32)...]
where the time goes in v3:
time: 96.1 us; the launch traced here: 95.8 us
  Pallas kernels  95.2 us (99%)
    pallas_call x1, Pallas kernels, body(): pl.pallas_call(kernel, out_shape=(jax.ShapeDtypeStruct((ROWS, COLS), F32)...  91.4 us
    pallas_call x1, Pallas kernels, body(): pl.pallas_call(finish, grid=(4,), out_shape=(jax.ShapeDtypeStruct((ROWS,...  3.8 us

profile of v3, /device:TPU:1, one launch (start us, length us, event | category | flops | bytes accessed | tf_op | source)
XLA Modules:
  0.0 95.8 jit_solution(10238653203752631615)
XLA Ops:
  0.6 91.4 %dual_step.1 = (f32[1024,256]{1,0:T(8,128)}, f32[8,256]{1,0:T(8,128)}) custom-call(s32[2,1024]{1,0:T(2,128)} %bitcast.3, s32[2,1024]{1,0:T(2,128)} %bitcast.4, f32[2,1024]{1,0:T(2,128)} %bitcast.5, s32[2,8]{1,0:T(2,128)} %near_list.1, s32[2,16]{1,0:T(2,128)} %far_list.1, bf16[64,512]{1,0:T(8,128)(2,1)} %top_ref.1, f32[2,1024,256]{2,1,0:T(8,128)} %basis_ref.1, ...), custom_call_target="tpu_custom_call" | custom-call | tf_op jit(solution)/shard_map/dual_step/pallas_call | solution.py:416
  92.0 3.8 %finish.1 = (f32[1024,256]{1,0:T(8,128)}, f32[3,256]{1,0:T(4,128)}) custom-call(f32[8,256]{1,0:T(8,128)} %get-tuple-element.4.total_ref, f32[2,1024,256]{2,1,0:T(8,128)} %basis_ref.1, f32[1024,256]{1,0:T(8,128)} %get-tuple-element.5.image_ref), custom_call_target="tpu_custom_call" | custom-call | tf_op jit(solution)/shard_map/finish/pallas_call | solution.py:455

commit v4 on v3

--- a/solution.py
+++ b/solution.py
@@ -20,6 +20,9 @@
 COLS = 256
 TOTAL = DEV * ROWS
 SELF = 2
+LIMIT_A = 57_000_000
+LIMIT_B = 4_000_000
+STEP = 128
 HELD = 12
 PARTS = 2
 WIDE = COLS // PARTS
@@ -42,7 +45,7 @@
     pick, place, slot_weight, slot_low, vec,
     send, got, reply, back,
     row_send, row_got,
-    acc, first, first_low, near_sum, dual_two, image, image_out,
+    acc, first, first_low, near_sum, dual_two, image,
     ag0, ag1, coeff, far_flat, far_in,
     par1, par2, tops, sums1, sums2,
     load_sem, send_sem, got_sem, row_send_sem, row_sem, reply_sem, back_sem,
@@ -344,33 +347,34 @@
     near_of(0, 1)
     gather(1, 0, 8)
     mid_a(0)
-    gather(1, 8, 16)
+    gather(1, 8, 12)
+    mid_b(0)
+    gather(1, 12, 16)
     early(1)
-    mid_b(0)
-    near_of(1, 0)
     mid_a(1)
     mid_c(0)
-    answer(0, 0, 8)
     mid_b(1)
-    answer(0, 8, 16)
+    answer(0, 0, 16)
+    near_of(1, 0)
     near_of(1, 1)
     mid_c(1)
     answer(1, 0, 16)
     loads[1].wait()
     v0, v1 = basis[0], basis[1]
     mutual = [jnp.sum(a * b, axis=0, keepdims=True) for a, b in ((v0, v0), (v0, v1), (v1, v1))]
-    collect(0)
-    collect(1)
-
-    found = jnp.concatenate([image[0], image[1]], axis=1)
-    image_out[...] = found
-    cross = [jnp.sum(basis[k] * found, axis=0, keepdims=True) for k in range(2)]
-    whole = jnp.sum(found * found, axis=0, keepdims=True)
-    sums1[group] = jnp.concatenate(cross + [whole] + mutual + [jnp.zeros((2, COLS), F32)], axis=0)
+    leaves, sums = [], []
+    for p in range(PARTS):
+        collect(p)
+        span = slice(p * WIDE, (p + 1) * WIDE)
+        leaves.append(pltpu.make_async_copy(image.at[p], image_hbm.at[:, pl.ds(p * WIDE, WIDE)], out_sem.at[p]))
+        leaves[p].start()
+        found = image[p]
+        sums.append([jnp.sum(basis[k, :, span] * found, axis=0, keepdims=True) for k in range(2)])
+        sums[p].append(jnp.sum(found * found, axis=0, keepdims=True))
+    sums = [jnp.concatenate([a, b], axis=1) for a, b in zip(*sums)]
+    sums1[group] = jnp.concatenate(sums + mutual + [jnp.zeros((2, COLS), F32)], axis=0)
     for k in range(1, 8):
         remote(sums1.at[group], sums1.at[group], sum_send_sem.at[0], sum_sem.at[0], (z, x, ys[k // 2], cs[k % 2]))
-    leave = pltpu.make_async_copy(image_out, image_hbm, out_sem)
-    leave.start()
     wait_for(sums1.at[pl.ds(0, 7)], sum_sem.at[0])
     sums2[branch] = jnp.sum(sums1[...], axis=0)
     for k in range(1, 16):
@@ -386,7 +390,8 @@
         for n in range(4):
             wait_for(par1.at[p, 0, three], par_send_sem.at[p, n])
         wait_for(tops.at[p, pl.ds(0, 7)], top_send_sem.at[p])
-    leave.wait()
+    for leave in leaves:
+        leave.wait()
     wait_for(sums1.at[pl.ds(0, 7)], sum_send_sem.at[0])
     wait_for(sums2.at[pl.ds(0, 15)], sum_sem.at[1])
     wait_for(sums2.at[pl.ds(0, 15)], sum_send_sem.at[1])
@@ -398,10 +403,17 @@
     total_ref[...] = jnp.concatenate([p0, p1, norm, 1.0 / norm, jnp.zeros((4, COLS), F32)], axis=0)
 
 
-def finish(total_ref, basis_ref, image_ref, out_ref, hess_ref):
+def finish(total_ref, basis, image, out_hbm, hess_ref, out, out_sem):
     p0, p1, scale = total_ref[0:1], total_ref[1:2], total_ref[3:4]
-    out_ref[...] = (image_ref[...] - (p0 * basis_ref[0] + p1 * basis_ref[1])) * scale
     hess_ref[...] = total_ref[0:3]
+    stores = []
+    for n in range(ROWS // STEP):
+        at = pl.ds(n * STEP, STEP)
+        out[at] = (image[at] - (p0 * basis[0, at] + p1 * basis[1, at])) * scale
+        stores.append(pltpu.make_async_copy(out.at[at], out_hbm.at[at], out_sem.at[n]))
+        stores[n].start()
+    for store in stores:
+        store.wait()
 
 
 def body(
@@ -433,35 +445,33 @@
             V((DEV, 1, 128), F32), V((DEV, 1, 128), F32),
             V((PARTS, ROWS, WIDE), F32), V((PARTS, ROWS, WIDE), F32), V((PARTS, 2, LEAF, WIDE), BF16),
             V((PARTS, ROWS, WIDE), F32), V((PARTS, ROWS, 2 * WIDE), BF16), V((PARTS, ROWS, WIDE), F32),
-            V((ROWS, COLS), F32),
             V((PARTS, 4, 4, RANK, WIDE), BF16), V((PARTS, 4, 4, RANK, WIDE), BF16), V((32, RANK, WIDE), BF16),
             V((2, RANK, 16 * RANK), BF16), V((16 * RANK, WIDE), BF16),
             V((PARTS, 2, 4, RANK // 2, WIDE), BF16), V((PARTS, 2, 4, RANK // 2, WIDE), BF16),
             V((PARTS, 8, RANK, WIDE), BF16), V((8, 8, COLS), F32), V((16, 8, COLS), F32),
             dma((8,)), dma((PARTS,)), dma((PARTS, 16)), dma, dma((16,)), dma((PARTS,)), dma((PARTS, 16)),
             dma((PARTS, 4)), dma((PARTS, 4)), dma((PARTS, 4)), dma((PARTS, 4)), dma((PARTS,)), dma((PARTS,)),
-            dma((2,)), dma((2,)), dma,
+            dma((2,)), dma((2,)), dma((PARTS,)),
         ],
         compiler_params=pltpu.CompilerParams(
-            collective_id=0, has_side_effects=True, vmem_limit_bytes=67_000_000
+            collective_id=0, has_side_effects=True, vmem_limit_bytes=LIMIT_A
         ),
         name="dual_step",
     )(
         spread_owner.T, spread_row.T, spread_weight.T, near_list, far_list, top_block,
         basis, gram_term, near_block, leaf_basis, far_block, ascend, descend,
     )
-    rows = ROWS // 4
+    parts = ROWS // STEP
     return tuple(
         pl.pallas_call(
             finish,
-            grid=(4,),
             out_shape=(jax.ShapeDtypeStruct((ROWS, COLS), F32), jax.ShapeDtypeStruct((3, COLS), F32)),
-            in_specs=[
-                pl.BlockSpec((8, COLS), lambda i: (0, 0)),
-                pl.BlockSpec((2, rows, COLS), lambda i: (0, i, 0)),
-                pl.BlockSpec((rows, COLS), lambda i: (i, 0)),
+            in_specs=[vmem, vmem, vmem],
+            out_specs=(hbm, vmem),
+            scratch_shapes=[
+                V((ROWS, COLS), F32), dma((parts,)),
             ],
-            out_specs=(pl.BlockSpec((rows, COLS), lambda i: (i, 0)), pl.BlockSpec((3, COLS), lambda i: (0, 0))),
+            compiler_params=pltpu.CompilerParams(vmem_limit_bytes=LIMIT_B),
             name="finish",
         )(total, basis, image)
     )

time: 96.1 us -> 95.4 us (level)
  Pallas kernels: 95.2 us -> 92.4 us
  local copies, waits for them, and re-layouts: 0 us -> 1.92 us
    pallas_call x1, Pallas kernels: 3.8 us -> 1.64 us  [body(): pl.pallas_call(finish, out_shape=(jax.ShapeDtypeStruct((ROWS, COLS), F32)...]
    unnamed x0 -> x6, local copies, waits for them, and re-layouts: none -> 1.92 us
where the time goes in v4:
time: 95.4 us; the launch traced here: 95.2 us
  Pallas kernels  92.4 us (97%)
  local copies, waits for them, and re-layouts  1.92 us (2%)
    pallas_call x1, Pallas kernels, body(): pl.pallas_call(kernel, out_shape=(jax.ShapeDtypeStruct((ROWS, COLS), F32)...  90.8 us
    unnamed x6, local copies, waits for them, and re-layouts  1.92 us

profile of v4, /device:TPU:1, one launch (start us, length us, event | category | flops | bytes accessed | tf_op | source)
XLA Modules:
  0.0 95.2 jit_solution(9797576082197741266)
XLA Ops:
  0.6 0.0 copy-start
  0.6 90.8 %dual_step.1 = (f32[1024,256]{1,0:T(8,128)}, f32[8,256]{1,0:T(8,128)}) custom-call(s32[2,1024]{1,0:T(2,128)} %bitcast.3, s32[2,1024]{1,0:T(2,128)} %bitcast.4, f32[2,1024]{1,0:T(2,128)} %bitcast.5, s32[2,8]{1,0:T(2,128)} %near_list.1, s32[2,16]{1,0:T(2,128)} %far_list.1, bf16[64,512]{1,0:T(8,128)(2,1)} %top_ref.1, f32[2,1024,256]{2,1,0:T(8,128)} %basis.1, ...), custom_call_target="tpu_custom_call" | custom-call | tf_op jit(solution)/shard_map/dual_step/pallas_call | solution.py:428
  91.4 0.0 copy-done
  91.4 0.0 copy-start.1
  91.4 1.2 %copy-done.1 = f32[1024,256]{1,0:T(8,128)S(1)} copy-done((f32[1024,256]{1,0:T(8,128)S(1)}, f32[1024,256]{1,0:T(8,128)}, u32[]{:S(2)}) %copy-start.1) | copy-done | bytes 1048600
  92.7 0.0 copy-start.2
  92.7 0.7 copy-done.2
  93.4 1.6 %finish.1 = (f32[1024,256]{1,0:T(8,128)}, f32[3,256]{1,0:T(4,128)}) custom-call(f32[8,256]{1,0:T(8,128)S(1)} %copy-done.2, f32[2,1024,256]{2,1,0:T(8,128)S(1)} %copy-done, f32[1024,256]{1,0:T(8,128)S(1)} %copy-done.1), custom_call_target="tpu_custom_call" | custom-call | tf_op jit(solution)/shard_map/finish/pallas_call | solution.py:466
Async XLA Ops:
  0.6 90.8 %copy-start = (f32[2,1024,256]{2,1,0:T(8,128)S(1)}, f32[2,1024,256]{2,1,0:T(8,128)}, u32[]{:S(2)}) copy-start(f32[2,1024,256]{2,1,0:T(8,128)} %basis.1) | copy-start | bytes 6291460
  91.4 1.2 %copy-start.1 = (f32[1024,256]{1,0:T(8,128)S(1)}, f32[1024,256]{1,0:T(8,128)}, u32[]{:S(2)}) copy-start(f32[1024,256]{1,0:T(8,128)} %get-tuple-element.5.image) | copy-start | bytes 3145732
  92.7 0.7 copy-start.2
